TPU v7x, 32 devices: a whole 2x2x4 slice. The times are simulated.
32 devices in a mesh: groups: 2 (over x), az: 16 (over z, y, core).
Axes of the slice: x: 2, y: 2, z: 4, core: 2. Of those that a mesh axis runs over, the one named last changes fastest.
Arguments:
- raw_first: bfloat16 [4, 8192, 8192], P('groups', 'az'), parts along dimension 0, may hold values from -6 to 6
- raw_second: bfloat16 [4, 8192, 8192], P('groups', 'az'), parts along dimension 0, may hold values from -6 to 6
- offsets: int32 [4], P('groups'), parts along dimension 0, may hold values from -16 to 16
- chirp_lengths: int32 [4], P('groups'), parts along dimension 0, may hold values from 256 to 2048
Outputs:
- interferogram: float32 [4, 1024, 8192], P('groups', 'az'), parts along dimension 0
- coherence: float32 [2048, 8192], P(('groups', 'az')), parts along dimension 0
There are 2 independent parts, one for each index of `groups`. A program takes and returns all parts, laid end to end along the dimension named above; each array names one. Nothing has to cross between parts.
Inputs may be any that keep to these rules, and one draw needn't show every extreme that they name: offsets[0] shifts azimuth lines, offsets[1] range bins. chirp_lengths[0] is the range chirp, chirp_lengths[1] the azimuth chirp.
All inputs are finite; a program needn't handle non-finite values.
Results may differ from a plain program's by a relative error of at most 0.0003.
Values sent between devices are 32-bit elements; how exact they have to be, the bound alone decides.
No kernel may reach another device: no remote copies, remote signals or barrier semaphores. Data moves between devices by JAX's collectives and lax.ppermute only.
A program may use at most 256 MiB of HBM per device.

v0:
```python
import math

import jax
import jax.numpy as jnp
from jax import lax
from jax.sharding import PartitionSpec as P

WINDOW = 1024
MAXSHIFT = 16


along_forms = (
    ("rij", "ik", "rkj"),
    ("rkj", "jl", "rkl"),
    ("rkl", "jl", "rkj"),
    ("rkj", "ik", "rij"),
)
turning_forms = (
    ("rij", "ik", "rkj"),
    ("rkj", "jl", "rkl"),
    ("rkl", "jl", "rkj"),
    ("rkj", "ik", "ijr"),
)


def padded_2(block, sides, width):
    for axis, dim in sides:
        count = lax.axis_size(axis)
        forward = [(i, i + 1) for i in range(count - 1)]
        backward = [(target, source) for source, target in forward]
        low = lax.ppermute(
            lax.slice_in_dim(block, block.shape[dim] - width, None, axis=dim), axis, forward
        )
        high = lax.ppermute(lax.slice_in_dim(block, 0, width, axis=dim), axis, backward)
        block = jnp.concatenate([low, block, high], axis=dim)
    return block


def chirp(length, samples_all):
    sample = jnp.arange(samples_all, dtype=jnp.int32)
    offset = 2 * sample - length
    period = 8 * length
    numerator = jnp.mod(offset * offset, period)
    angles = jnp.pi * numerator.astype(jnp.float32) / (4 * length).astype(jnp.float32)
    amplitude = jnp.where(sample < length, 1.0 / jnp.sqrt(length.astype(jnp.float32)), 0.0)
    return (amplitude * jnp.cos(angles), amplitude * jnp.sin(angles))


def roots(rows_count, cols_count, period):
    product = lax.broadcasted_iota(jnp.int32, (rows_count, cols_count), 0) * lax.broadcasted_iota(
        jnp.int32, (rows_count, cols_count), 1
    )
    angles = -2.0 * math.pi / period * jnp.mod(product, period).astype(jnp.float32)
    return (jnp.cos(angles), jnp.sin(angles))


def tables(length):
    left_size = math.isqrt(length)
    while length % left_size:
        left_size -= 1
    right_size = length // left_size
    entries = (
        roots(left_size, left_size, left_size)
        + roots(right_size, right_size, right_size)
        + roots(left_size, right_size, length)
    )
    return (entries, left_size, right_size)


def complex_product(form, stacked, table_real, table_imag):
    left_side, right_side, result_side = form
    matrix = jnp.stack([jnp.stack([table_real, table_imag]), jnp.stack([-table_imag, table_real])])
    return jnp.einsum(
        "c" + left_side + ",cd" + right_side + "->d" + result_side,
        stacked,
        matrix,
        precision=lax.Precision.HIGHEST,
    )


def complex_times(stacked, other_real, other_imag):
    return jnp.stack(
        [
            stacked[0] * other_real - stacked[1] * other_imag,
            stacked[0] * other_imag + stacked[1] * other_real,
        ]
    )


def forward(stacked, entries, forms):
    left_real, left_imag, right_real, right_imag, twist_real, twist_imag = entries
    stacked = complex_product(forms[0], stacked, left_real, left_imag)
    stacked = complex_times(stacked, twist_real, twist_imag)
    return complex_product(forms[1], stacked, right_real, right_imag)


def inverse(stacked, entries, forms, keep):
    left_real, left_imag, right_real, right_imag, twist_real, twist_imag = entries
    stacked = complex_product(forms[2], stacked, right_real, -right_imag)
    stacked = complex_times(stacked, twist_real, -twist_imag)
    stacked = complex_product(forms[3], stacked, left_real[0:keep], -left_imag[0:keep])
    return stacked * (1.0 / twist_real.size)


def products(fields):
    return jnp.stack(
        [
            fields[0] * fields[2] + fields[1] * fields[3],
            fields[1] * fields[2] - fields[0] * fields[3],
            fields[0] * fields[0] + fields[1] * fields[1],
            fields[2] * fields[2] + fields[3] * fields[3],
        ]
    )


def azimuth_box(values):
    lines_all = values.shape[2]
    padded = jnp.pad(values, ((0, 0), (0, 0), (3, 4)))
    result = padded[:, :, 0:lines_all]
    for offset_line in range(1, 8):
        result = result + padded[:, :, offset_line : offset_line + lines_all]
    return result


def range_box(extended, bins_count):
    result = extended[:, 1 : 1 + bins_count]
    for offset_bin in range(2, 9):
        result = result + extended[:, offset_bin : offset_bin + bins_count]
    return result


def on_device(raw_first, raw_second, offsets, chirp_lengths):
    lines_count = raw_first.shape[1]
    range_count = raw_first.shape[2]
    azimuth_count = lines_count * lax.axis_size("az")
    range_tables, range_left, range_right = tables(range_count)
    azimuth_tables, azimuth_left, azimuth_right = tables(azimuth_count)
    range_keep = -(-(WINDOW + MAXSHIFT) // range_right)
    chirp_real, chirp_imag = chirp(chirp_lengths[0], range_count)
    range_spec = forward(
        jnp.stack([chirp_real, chirp_imag]).reshape(2, 1, range_left, range_right),
        range_tables,
        along_forms,
    )
    chirp_real, chirp_imag = chirp(chirp_lengths[1], azimuth_count)
    azimuth_spec = forward(
        jnp.stack([chirp_real, chirp_imag]).reshape(2, 1, azimuth_left, azimuth_right),
        azimuth_tables,
        along_forms,
    )

    def range_focus(raw):
        stacked = raw.astype(jnp.float32).reshape(2, lines_count, range_left, range_right)
        stacked = forward(stacked, range_tables, turning_forms)
        stacked = complex_times(stacked, range_spec[0, 0], -range_spec[1, 0])
        stacked = inverse(stacked, range_tables, turning_forms, range_keep)
        return stacked.reshape(2, range_keep * range_right, lines_count)

    def azimuth_focus(paired):
        bins_count = paired.shape[1]
        stacked = paired.reshape(2, bins_count, azimuth_left, azimuth_right)
        stacked = forward(stacked, azimuth_tables, along_forms)
        stacked = complex_times(stacked, azimuth_spec[0, 0], -azimuth_spec[1, 0])
        stacked = inverse(stacked, azimuth_tables, along_forms, azimuth_left)
        return stacked.reshape(2, bins_count, azimuth_count)

    first_ranged = range_focus(raw_first)[:, 0:WINDOW]
    padded = jnp.pad(range_focus(raw_second), ((0, 0), (MAXSHIFT, 0), (0, 0)))
    second_ranged = lax.dynamic_slice_in_dim(padded, MAXSHIFT - offsets[1], WINDOW, 1)
    first_turned, second_turned = (
        lax.all_to_all(first_ranged, "az", split_axis=1, concat_axis=2, tiled=True),
        lax.all_to_all(second_ranged, "az", split_axis=1, concat_axis=2, tiled=True),
    )
    first_image = azimuth_focus(first_turned)
    second_image = azimuth_focus(second_turned)
    padded = jnp.pad(second_image, ((0, 0), (0, 0), (MAXSHIFT, MAXSHIFT)))
    second_image = lax.dynamic_slice_in_dim(padded, MAXSHIFT - offsets[0], azimuth_count, 2)
    bins_count = first_image.shape[1]
    fields = jnp.concatenate([first_image, second_image], axis=0)
    partial_sums = azimuth_box(products(fields))
    extended = padded_2(partial_sums, (("az", 1),), 4)
    sums = range_box(extended, bins_count)
    coherence = jnp.sqrt(sums[0] * sums[0] + sums[1] * sums[1]) / jnp.sqrt(sums[2] * sums[3] + 1.0)
    interferogram = sums[0:2] / 64.0
    return (interferogram, coherence)


def solution(mesh):
    in_specs = (P("groups", "az", None), P("groups", "az", None), P("groups"), P("groups"))
    out_specs = (P("groups", "az", None), P(("groups", "az"), None))
    return jax.shard_map(
        on_device, mesh=mesh, in_specs=in_specs, out_specs=out_specs, check_vma=False
    )
```

profile of v0, /device:TPU:17, one launch (start us, length us, event | category | flops | bytes accessed | tf_op | source)
XLA Modules:
  0.0 952.6 jit_solution(535527850417652346)
XLA Ops:
  10.4 15.1 %copy.165 = bf16[128,8,64,128]{3,2,1,0:T(8,128)(2,1)} copy(bf16[128,8,64,128]{3,1,2,0:T(8,128)(2,1)} %bitcast.340) | data formatting | bytes 33554432
  25.5 22.6 %convolution_bitcast_fusion = f32[2,512,64,128]{3,2,1,0:T(8,128)} fusion(f32[1,2,64,64]{2,3,0,1:T(8,128)S(1)} %get-tuple-element.51, f32[1,2,64,64]{2,3,0,1:T(8,128)S(1)} %get-tuple-element.64, bf16[2,512,64,128]{3,2,1,0:T(8,128)(2,1)} %bitcast.336), kind=kOutput, calls=%fused_computation.21 | convolution fusion | flops 12884918272 | bytes 50397184 | tf_op jit(solution)/shard_map/crij,cdik->drkj/dot_general | solution.py:73
  48.1 15.1 %copy.164 = bf16[128,8,64,128]{3,2,1,0:T(8,128)(2,1)} copy(bf16[128,8,64,128]{3,1,2,0:T(8,128)(2,1)} %bitcast.341) | data formatting | bytes 33554432
  63.2 23.1 %convolution_bitcast_fusion.1 = f32[2,512,64,128]{3,2,1,0:T(8,128)} fusion(f32[1,2,64,64]{2,3,0,1:T(8,128)S(1)} %get-tuple-element.51, f32[1,2,64,64]{2,3,0,1:T(8,128)S(1)} %get-tuple-element.64, bf16[2,512,64,128]{3,2,1,0:T(8,128)(2,1)} %bitcast.337), kind=kOutput, calls=%fused_computation.22 | convolution fusion | flops 12884918272 | bytes 50397184 | tf_op jit(solution)/shard_map/crij,cdik->drkj/dot_general | solution.py:73
  86.4 47.7 %multiply_subtract_fusion.5 = (f32[1,512,64,128]{3,2,1,0:T(8,128)}, f32[1,512,64,128]{3,2,1,0:T(8,128)}, f32[1,512,64,128]{3,2,1,0:T(8,128)}, f32[1,512,64,128]{3,2,1,0:T(8,128)}) fusion(f32[2,512,64,128]{3,2,1,0:T(8,128)} %convolution_bitcast_fusion.1, f32[64,128]{1,0:T(8,128)S(1)} %get-tuple-element.77, f32[64,128]{1,0:T(8,128)S(1)} %get-tuple-element.78, ...), kind=kLoop, calls=%fused_computation.42 | loop fusion | flops 50331648 | bytes 134283264 | tf_op jit(solution)/shard_map/sub | solution.py:84
  134.0 23.5 %pad_maximum_fusion.2 = f32[2,512,64,128]{3,2,1,0:T(8,128)} fusion(f32[1,512,64,128]{3,2,1,0:T(8,128)} %get-tuple-element.48, f32[1,512,64,128]{3,2,1,0:T(8,128)} %get-tuple-element.49), kind=kLoop, calls=%fused_computation.3 | loop fusion | flops 8388608 | bytes 67108864 | tf_op jit(solution)/shard_map/stack | solution.py:82
  157.5 58.2 %fusion.15 = f32[2,512,64,128]{1,3,2,0:T(8,128)} fusion(f32[2,512,64,128]{3,2,1,0:T(8,128)} %pad_maximum_fusion.2, f32[1,2,128,128]{2,3,0,1:T(8,128)S(1)} %get-tuple-element.35, f32[1,2,128,128]{2,3,0,1:T(8,128)S(1)} %get-tuple-element.58), kind=kOutput, calls=%fused_computation.26 | convolution fusion | flops 25769869312 | bytes 67371008 | tf_op jit(solution)/shard_map/crkj,cdjl->drkl/dot_general | solution.py:73
  215.8 23.5 %pad_maximum_fusion = f32[2,512,64,128]{3,2,1,0:T(8,128)} fusion(f32[1,512,64,128]{3,2,1,0:T(8,128)} %get-tuple-element.7, f32[1,512,64,128]{3,2,1,0:T(8,128)} %get-tuple-element.6), kind=kLoop, calls=%fused_computation | loop fusion | flops 8388608 | bytes 67108864 | tf_op jit(solution)/shard_map/stack | solution.py:82
  239.3 58.5 %fusion.12 = f32[2,512,64,128]{1,3,2,0:T(8,128)} fusion(f32[2,512,64,128]{3,2,1,0:T(8,128)} %pad_maximum_fusion, f32[1,2,128,128]{2,3,0,1:T(8,128)S(1)} %get-tuple-element.35, f32[1,2,128,128]{2,3,0,1:T(8,128)S(1)} %get-tuple-element.58), kind=kOutput, calls=%fused_computation.25 | convolution fusion | flops 25769869312 | bytes 67371008 | tf_op jit(solution)/shard_map/crkj,cdjl->drkl/dot_general | solution.py:73
  297.8 45.5 %multiply_subtract_fusion.4 = (f32[1,512,64,128]{1,3,2,0:T(8,128)}, f32[1,512,64,128]{1,3,2,0:T(8,128)}, f32[1,512,64,128]{1,3,2,0:T(8,128)}, f32[1,512,64,128]{1,3,2,0:T(8,128)}) fusion(f32[2,512,64,128]{1,3,2,0:T(8,128)} %fusion.12, f32[64,128]{1,0:T(8,128)S(1)} %copy-done.20, f32[64,128]{1,0:T(8,128)S(1)} %copy-done.19, f32[2,512,64,128]{1,3,2,0:T(8,128)} %fusion.15), kind=kLoop, calls=%fused_computation.40 | loop fusion | flops 50331648 | bytes 134283264 | tf_op jit(solution)/shard_map/sub | solution.py:84
  343.3 23.5 %maximum_bitcast_fusion.1 = f32[2,512,64,128,1]{1,3,2,0,4:T(8,128)} fusion(f32[1,512,64,128]{1,3,2,0:T(8,128)} %get-tuple-element.46, f32[1,512,64,128]{1,3,2,0:T(8,128)} %get-tuple-element.47), kind=kLoop, calls=%fused_computation.4 | loop fusion | flops 8388608 | bytes 67108864 | tf_op jit(solution)/shard_map/stack | solution.py:82
  366.8 32.2 %copy.132 = f32[2,512,64,128,1]{3,2,0,1,4:T(8,128)} copy(f32[2,512,64,128,1]{1,3,2,0,4:T(8,128)} %maximum_bitcast_fusion.1) | data formatting | bytes 67108864 | tf_op jit(solution)/shard_map/stack | solution.py:82
  399.0 23.5 %maximum_bitcast_fusion = f32[2,512,64,128,1]{1,3,2,0,4:T(8,128)} fusion(f32[1,512,64,128]{1,3,2,0:T(8,128)} %get-tuple-element.5, f32[1,512,64,128]{1,3,2,0:T(8,128)} %get-tuple-element.4), kind=kLoop, calls=%fused_computation.1 | loop fusion | flops 8388608 | bytes 67108864 | tf_op jit(solution)/shard_map/stack | solution.py:82
  422.5 32.3 %copy.115 = f32[2,512,64,128,1]{3,2,0,1,4:T(8,128)} copy(f32[2,512,64,128,1]{1,3,2,0,4:T(8,128)} %maximum_bitcast_fusion) | data formatting | bytes 67108864 | tf_op jit(solution)/shard_map/stack | solution.py:82
  454.8 32.8 %convolution_bitcast_fusion.2 = f32[2,512,64,128]{3,2,1,0:T(8,128)} fusion(f32[2,512,64,128,1]{3,2,0,1,4:T(8,128)} %copy.132, f32[1,2,128,128]{2,3,1,0:T(8,128)S(1)} %copy-done.7, f32[1,2,128,128]{2,3,1,0:T(8,128)S(1)} %copy-done.6), kind=kOutput, calls=%fused_computation.23 | convolution fusion | flops 25769869312 | bytes 67371008 | tf_op jit(solution)/shard_map/crkl,cdjl->drkj/dot_general | solution.py:73
  487.6 32.7 %convolution_bitcast_fusion.3 = f32[2,512,64,128]{3,2,1,0:T(8,128)} fusion(f32[2,512,64,128,1]{3,2,0,1,4:T(8,128)} %copy.115, f32[1,2,128,128]{2,3,1,0:T(8,128)S(1)} %copy-done.7, f32[1,2,128,128]{2,3,1,0:T(8,128)S(1)} %copy-done.6), kind=kOutput, calls=%fused_computation.24 | convolution fusion | flops 25769869312 | bytes 67371008 | tf_op jit(solution)/shard_map/crkl,cdjl->drkj/dot_general | solution.py:73
  521.1 47.9 %multiply_subtract_fusion.3 = (f32[1,512,64,128]{3,2,1,0:T(8,128)}, f32[1,512,64,128]{3,2,1,0:T(8,128)}, f32[1,512,64,128]{3,2,1,0:T(8,128)}, f32[1,512,64,128]{3,2,1,0:T(8,128)}) fusion(f32[2,512,64,128]{3,2,1,0:T(8,128)} %convolution_bitcast_fusion.3, f32[64,128]{1,0:T(8,128)S(1)} %copy-done.16, f32[64,128]{1,0:T(8,128)S(1)} %copy-done.13, ...), kind=kLoop, calls=%fused_computation.38 | loop fusion | flops 50331648 | bytes 134283264 | tf_op jit(solution)/shard_map/sub | solution.py:84
  569.0 22.1 %fusion.34 = f32[2,9,128,512]{2,1,3,0:T(8,128)} fusion(f32[1,2,9,64]{3,2,0,1:T(8,128)S(1)} %get-tuple-element.70, f32[1,2,9,64]{3,2,0,1:T(8,128)S(1)} %get-tuple-element.69, f32[1,512,64,128]{3,2,1,0:T(8,128)} %get-tuple-element.44, f32[1,512,64,128]{3,2,1,0:T(8,128)} %get-tuple-element.45), kind=kOutput, calls=%fused_computation.66 | convolution fusion | flops 1821509888 | bytes 38282240 | tf_op jit(solution)/shard_map/crkj,cdik->dijr/dot_general | solution.py:73
  591.1 8.5 copy.97
  604.2 5.2 copy.98
  609.4 7.0 all-to-all-start.1
  616.4 22.1 %fusion.35 = f32[2,9,128,512]{2,1,3,0:T(8,128)} fusion(f32[1,2,9,64]{3,2,0,1:T(8,128)S(1)} %get-tuple-element.70, f32[1,2,9,64]{3,2,0,1:T(8,128)S(1)} %get-tuple-element.69, f32[1,512,64,128]{3,2,1,0:T(8,128)} %get-tuple-element.3, f32[1,512,64,128]{3,2,1,0:T(8,128)} %get-tuple-element.2), kind=kOutput, calls=%fused_computation.68 | convolution fusion | flops 1821509888 | bytes 38282240 | tf_op jit(solution)/shard_map/crkj,cdik->dijr/dot_general | solution.py:73
  638.5 8.5 copy.80
  649.6 5.2 copy.81
  654.9 53.5 %all-to-all-done.1 = f32[2,1024,512]{2,0,1:T(2,128)} async-done(((f32[2,1024,512]{2,0,1:T(2,128)}), f32[2,1024,512]{2,0,1:T(2,128)}, u32[]{:S(2)}, u32[]{:S(2)}) %all-to-all-start.1) | async-done | bytes 4194336 | tf_op jit(solution)/shard_map/all_to_all | solution.py:172
  708.4 5.5 all-to-all-start
  718.9 3.0 copy.99
  721.9 4.4 copy.100
  726.3 4.8 reshape.501
  731.2 8.0 convolution_bitcast_fusion.4
  739.1 66.6 %all-to-all-done = f32[2,1024,512]{2,0,1:T(2,128)} async-done(((f32[2,1024,512]{2,0,1:T(2,128)}), f32[2,1024,512]{2,0,1:T(2,128)}, u32[]{:S(2)}, u32[]{:S(2)}) %all-to-all-start) | async-done | bytes 4194336 | tf_op jit(solution)/shard_map/all_to_all | solution.py:171
  805.8 3.0 copy.82
  808.8 4.4 copy.83
  813.2 4.7 reshape.477
  817.9 5.9 convolution_bitcast_fusion.5
  825.9 3.8 fusion.67
  829.7 3.7 fusion.61
  835.5 4.2 fusion.70
  839.7 3.8 fusion.64
  846.4 5.6 fusion.37
  852.0 5.1 reshape.460
  857.1 5.4 fusion.44
  869.3 12.1 %multiply_add_fusion.8 = (f32[1,64,8192]{2,1,0:T(8,128)}, f32[1,64,8192]{2,1,0:T(8,128)}, f32[1,64,8192]{2,1,0:T(8,128)}, f32[1,64,8192]{2,1,0:T(8,128)}) fusion(f32[1,64,8192]{2,1,0:T(8,128)} %squeeze.11, f32[1,64,8192]{2,1,0:T(8,128)S(1)} %squeeze.10, s32[]{:T(128)S(6)} %select_n.278, f32[2,64,8192]{2,1,0:T(8,128)} %reshape.460, s32[]{:T(128)S(6)} %add.431), kind=kLoop, calls=%fused_computation.123 | loop fusion | flops 6291456 | bytes 16777224 | tf_op jit(solution)/shard_map/add | solution.py:108
  881.3 3.8 pad_maximum_fusion.6
  885.2 15.4 %slice_add_fusion = f32[4,64,8192]{2,1,0:T(8,128)S(1)} fusion(f32[4,64,8192]{2,1,0:T(8,128)S(1)} %pad_maximum_fusion.6), kind=kLoop, calls=%fused_computation.69 | loop fusion | flops 14680064 | bytes 16777216 | tf_op jit(solution)/shard_map/add | solution.py:121
  905.8 8.8 collective-permute-done
  914.7 3.4 collective-permute-done.1
  918.1 29.7 %fusion.24 = f32[4,64,8192]{2,1,0:T(8,128)S(1)} fusion(f32[4,64,8192]{2,1,0:T(8,128)} %copy-done, f32[4,4,8192]{2,1,0:T(4,128)S(1)} %collective-permute-done, f32[4,4,8192]{2,1,0:T(4,128)S(1)} %collective-permute-done.1), kind=kLoop, calls=%fused_computation.52 | loop fusion | flops 29360128 | bytes 17825792 | tf_op jit(solution)/shard_map/add | solution.py:128
  (80 shorter events, 39.9 us)
Async XLA Ops:
  1.6 84.7 %copy-start.12 = (f32[64,128]{1,0:T(8,128)}, f32[64,128]{1,0:T(8,128)S(1)}, u32[]{:S(2)}) copy-start(f32[64,128]{1,0:T(8,128)S(1)} %get-tuple-element.78) | copy-start | bytes 98308
  1.6 84.7 %copy-start.17 = (f32[64,128]{1,0:T(8,128)}, f32[64,128]{1,0:T(8,128)S(1)}, u32[]{:S(2)}) copy-start(f32[64,128]{1,0:T(8,128)S(1)} %get-tuple-element.77) | copy-start | bytes 98308
  8.2 55.0 %copy-start.8 = (f32[1,2,64,64]{2,3,0,1:T(8,128)}, f32[1,2,64,64]{2,3,0,1:T(8,128)S(1)}, u32[]{:S(2)}) copy-start(f32[1,2,64,64]{2,3,0,1:T(8,128)S(1)} %get-tuple-element.51) | copy-start | bytes 98308
  8.2 55.0 %copy-start.10 = (f32[1,2,64,64]{2,3,0,1:T(8,128)}, f32[1,2,64,64]{2,3,0,1:T(8,128)S(1)}, u32[]{:S(2)}) copy-start(f32[1,2,64,64]{2,3,0,1:T(8,128)S(1)} %get-tuple-element.64) | copy-start | bytes 98308
  9.4 229.9 %copy-start.2 = (f32[1,2,128,128]{2,3,0,1:T(8,128)}, f32[1,2,128,128]{2,3,0,1:T(8,128)S(1)}, u32[]{:S(2)}) copy-start(f32[1,2,128,128]{2,3,0,1:T(8,128)S(1)} %get-tuple-element.35) | copy-start | bytes 393220
  9.4 229.9 %copy-start.4 = (f32[1,2,128,128]{2,3,0,1:T(8,128)}, f32[1,2,128,128]{2,3,0,1:T(8,128)S(1)}, u32[]{:S(2)}) copy-start(f32[1,2,128,128]{2,3,0,1:T(8,128)S(1)} %get-tuple-element.58) | copy-start | bytes 393220
  239.3 58.5 %copy-start.19 = (f32[64,128]{1,0:T(8,128)S(1)}, f32[64,128]{1,0:T(8,128)}, u32[]{:S(2)}) copy-start(f32[64,128]{1,0:T(8,128)} %get-tuple-element.60) | copy-start | bytes 98308
  239.3 58.5 %copy-start.20 = (f32[64,128]{1,0:T(8,128)S(1)}, f32[64,128]{1,0:T(8,128)}, u32[]{:S(2)}) copy-start(f32[64,128]{1,0:T(8,128)} %get-tuple-element.61) | copy-start | bytes 98308
  422.5 32.3 %copy-start.6 = (f32[1,2,128,128]{2,3,1,0:T(8,128)S(1)}, f32[1,2,128,128]{2,3,1,0:T(8,128)}, u32[]{:S(2)}) copy-start(f32[1,2,128,128]{2,3,1,0:T(8,128)} %get-tuple-element.34) | copy-start | bytes 393220
  422.5 32.3 %copy-start.7 = (f32[1,2,128,128]{2,3,1,0:T(8,128)S(1)}, f32[1,2,128,128]{2,3,1,0:T(8,128)}, u32[]{:S(2)}) copy-start(f32[1,2,128,128]{2,3,1,0:T(8,128)} %get-tuple-element.59) | copy-start | bytes 393220
  487.6 33.5 %copy-start.13 = (f32[64,128]{1,0:T(8,128)S(1)}, f32[64,128]{1,0:T(8,128)}, u32[]{:S(2)}) copy-start(f32[64,128]{1,0:T(8,128)} %copy-done.12) | copy-start | bytes 98308
  487.6 33.5 %copy-start.16 = (f32[64,128]{1,0:T(8,128)S(1)}, f32[64,128]{1,0:T(8,128)}, u32[]{:S(2)}) copy-start(f32[64,128]{1,0:T(8,128)} %fusion.172) | copy-start | bytes 98308
  591.1 8.5 copy-start.21
  609.4 98.9 %all-to-all-start.1 = ((f32[2,1024,512]{2,0,1:T(2,128)}), f32[2,1024,512]{2,0,1:T(2,128)}, u32[]{:S(2)}, u32[]{:S(2)}) async-start(f32[2,1024,512]{2,0,1:T(2,128)} %copy.98), calls=%async_computation.1 | async-start | bytes 8388608 | tf_op jit(solution)/shard_map/all_to_all | solution.py:172
  654.9 63.1 %copy-start.9 = (f32[1,2,64,64]{2,3,0,1:T(8,128)S(1)}, f32[1,2,64,64]{2,3,0,1:T(8,128)}, u32[]{:S(2)}) copy-start(f32[1,2,64,64]{2,3,0,1:T(8,128)} %copy-done.8) | copy-start | bytes 98308
  654.9 63.2 %copy-start.11 = (f32[1,2,64,64]{2,3,0,1:T(8,128)S(1)}, f32[1,2,64,64]{2,3,0,1:T(8,128)}, u32[]{:S(2)}) copy-start(f32[1,2,64,64]{2,3,0,1:T(8,128)} %copy-done.10) | copy-start | bytes 98308
  654.9 63.6 %copy-start.3 = (f32[1,2,128,128]{2,3,0,1:T(8,128)S(1)}, f32[1,2,128,128]{2,3,0,1:T(8,128)}, u32[]{:S(2)}) copy-start(f32[1,2,128,128]{2,3,0,1:T(8,128)} %copy-done.2) | copy-start | bytes 393220
  654.9 63.6 %copy-start.5 = (f32[1,2,128,128]{2,3,0,1:T(8,128)S(1)}, f32[1,2,128,128]{2,3,0,1:T(8,128)}, u32[]{:S(2)}) copy-start(f32[1,2,128,128]{2,3,0,1:T(8,128)} %copy-done.4) | copy-start | bytes 393220
  708.4 97.4 %all-to-all-start = ((f32[2,1024,512]{2,0,1:T(2,128)}), f32[2,1024,512]{2,0,1:T(2,128)}, u32[]{:S(2)}, u32[]{:S(2)}) async-start(f32[2,1024,512]{2,0,1:T(2,128)} %copy.81), calls=%async_computation | async-start | bytes 8388608 | tf_op jit(solution)/shard_map/all_to_all | solution.py:171
  817.9 5.9 copy-start.1
  817.9 5.9 copy-start.18
  843.5 2.9 copy-start.14
  843.5 2.9 copy-start.15
  900.6 14.1 %copy-start = (f32[4,64,8192]{2,1,0:T(8,128)}, f32[4,64,8192]{2,1,0:T(8,128)S(1)}, u32[]{:S(2)}) copy-start(f32[4,64,8192]{2,1,0:T(8,128)S(1)} %slice_add_fusion) | copy-start | bytes 25165828
  900.8 13.9 %collective-permute-start = (f32[4,4,8192]{2,1,0:T(4,128)S(1)}, f32[4,4,8192]{2,1,0:T(4,128)S(1)}, u32[]{:S(2)}, u32[]{:S(2)}) collective-permute-start(f32[4,4,8192]{2,1,0:T(4,128)S(1)} %get-tuple-element.15), channel_id=1, source_target_pairs={{0,1},{1,2},{2,3},{3,4},{4,5},{5,6},{6,7},{7,8},{8,9},{9,10},{10,1... | collective-permute-start | bytes 1572872 | tf_op jit(solution)/shard_map/ppermute | solution.py:31
  902.9 15.2 %collective-permute-start.1 = (f32[4,4,8192]{2,1,0:T(4,128)S(1)}, f32[4,4,8192]{2,1,0:T(4,128)S(1)}, u32[]{:S(2)}, u32[]{:S(2)}) collective-permute-start(f32[4,4,8192]{2,1,0:T(4,128)S(1)} %get-tuple-element.14), channel_id=1, source_target_pairs={{1,0},{2,1},{3,2},{4,3},{5,4},{6,5},{7,6},{8,7},{9,8},{10,9},{11,1... | collective-permute-start | bytes 1572872 | tf_op jit(solution)/shard_map/ppermute | solution.py:34
where the time goes:
time: 963 us; the launch traced here: 953 us
  other arithmetic  315 us (33%)
  matrix products  314 us (33%)
  local copies, waits for them, and re-layouts  166 us (17%)
  waiting for transfers between devices  132 us (14%)
  starting transfers between devices  17.5 us (2%)
    dot_general x20, matrix products, complex_product(): jnp.einsum('c' + left_side + ',cd' + right_side + '->d' + result_side, st...  314 us
    sub x6, other arithmetic, complex_times(): stacked[0] * other_real - stacked[1] * other_imag  148 us
    another operation x6, other arithmetic, complex_times(): jnp.stack([stacked[0] * other_real - stacked[1] * other_imag, stacked[0]...  94.3 us
    all_to_all x1, waiting for transfers between devices, on_device(): lax.all_to_all(first_ranged, 'az', split_axis=1, concat_axis=2, tiled=True)  66.6 us
    another operation x2, local copies, waits for them, and re-layouts, complex_times(): jnp.stack([stacked[0] * other_real - stacked[1] * other_imag, stacked[0]...  64.5 us
    all_to_all x1, waiting for transfers between devices, on_device(): lax.all_to_all(second_ranged, 'az', split_axis=1, concat_axis=2, tiled=True)  53.5 us
    unnamed x46, local copies, waits for them, and re-layouts  30.3 us
    add x1, other arithmetic, range_box(): result = result + extended[:, offset_bin:offset_bin + bins_count]  29.7 us
  transfers between devices with their start and end apart: 4, of which 4 were waited for; matrix products, arithmetic and copies ran while one was open for 6% of the time, Pallas kernels for 0%

commit v1 on v0

v1 whole, which is shorter than its diff:
```python
import functools
import math

import jax
import jax.numpy as jnp
from jax import lax
from jax.experimental import pallas as pl
from jax.experimental.pallas import tpu as pltpu
from jax.sharding import PartitionSpec as P

WINDOW = 1024
MAXSHIFT = 16
SPAN = 256
HALF = 128
LIMIT = 60 * 1024 * 1024

F32, BF16 = jnp.float32, jnp.bfloat16


def chirps(lengths, samples):
    sample = lax.broadcasted_iota(jnp.int32, (2, samples), 1)
    length = lengths[:, None]
    offset = 2 * sample - length
    numerator = jnp.mod(offset * offset, 8 * length)
    angles = jnp.pi * numerator.astype(F32) / (4 * length).astype(F32)
    amplitude = jnp.where(sample < length, 1.0 / jnp.sqrt(length.astype(F32)), 0.0)
    return amplitude * jnp.cos(angles), amplitude * jnp.sin(angles)


def table_kernel(plan, offs_ref, real_ref, imag_ref, *refs):
    outs, scratch = refs[:-1], refs[-1]
    for (row, which, lead, depth, starts), out in zip(plan, outs):
        cols = 8 * len(starts)
        base = lead - offs_ref[which] if lead else 0
        for part, ref in enumerate((real_ref, imag_ref)):
            line = jnp.broadcast_to(ref[row : row + 1, 0:depth], (8, depth))
            line = pltpu.roll(line, 0, 1, stride=1, stride_axis=0)
            uniform = all(start == 8 * k for k, start in enumerate(starts))
            if uniform and len(starts) > 8:

                @pl.loop(0, len(starts))
                def _(k):
                    moved = pltpu.roll(line, base + 8 * k, 1)
                    scratch[pl.ds(pl.multiple_of(part * cols + 8 * k, 8), 8), 0:depth] = moved

            else:
                for k, start in enumerate(starts):
                    moved = pltpu.roll(line, base + start, 1)
                    scratch[part * cols + 8 * k : part * cols + 8 * k + 8, 0:depth] = moved

        @pl.loop(0, depth // HALF)
        def _(k):
            at = pl.ds(pl.multiple_of(k * HALF, HALF), HALF)
            turned = scratch[0 : 2 * cols, at].T
            high = turned.astype(BF16)
            out[at, 0 : 2 * cols] = high
            out[at, 2 * cols : 4 * cols] = (turned - high.astype(F32)).astype(BF16)


def make_tables(plan, offsets, real, imag):
    rows = max(2 * 8 * len(item[4]) for item in plan)
    depth = max(item[3] for item in plan)
    size = sum(item[3] * 32 * len(item[4]) for item in plan)
    vmem = pl.BlockSpec(memory_space=pltpu.VMEM)
    return pl.pallas_call(
        functools.partial(table_kernel, plan),
        out_shape=[jax.ShapeDtypeStruct((item[3], 32 * len(item[4])), BF16) for item in plan],
        in_specs=[pl.BlockSpec(memory_space=pltpu.SMEM), vmem, vmem],
        out_specs=[vmem] * len(plan),
        scratch_shapes=[pltpu.VMEM((rows, depth), F32)],
        compiler_params=pltpu.CompilerParams(vmem_limit_bytes=LIMIT),
        cost_estimate=pl.CostEstimate(flops=size * 200, bytes_accessed=2 * size, transcendentals=0),
        name="tables",
    )(offsets, real, imag)


def range_kernel(plan, sizes, offs_ref, first_ref, second_ref, *refs):
    tables, out = refs[0:2], refs[2]
    windows, share, bins = sizes
    lines = out.shape[3]
    cols = share * len(bins) * 8
    for side, (source, table) in enumerate(zip((first_ref, second_ref), tables)):
        lead, depth = plan[side]

        def piece(start, stop):
            return source[:, :, start:stop].reshape(2 * lines, stop - start)

        for window in range(windows):
            start = SPAN * window - lead
            if start < 0:
                left = jnp.concatenate(
                    [jnp.zeros((2 * lines, -start), BF16), piece(0, start + depth)], axis=1
                )
            else:
                left = piece(start, start + depth)
            both = jnp.dot(left, table[...], preferred_element_type=F32)
            turned = (both[:, 0 : 2 * cols] + both[:, 2 * cols :]).T
            real = turned[0:cols, 0:lines] + turned[cols:, lines:]
            imag = turned[0:cols, lines:] - turned[cols:, 0:lines]
            real = real.reshape(share, len(bins) * 8, lines)
            imag = imag.reshape(share, len(bins) * 8, lines)
            if side and start < 0:
                shape = (share, 8, lines)
                own = lax.broadcasted_iota(jnp.int32, shape, 0) * (SPAN // share)
                own = own + lax.broadcasted_iota(jnp.int32, shape, 1)
                index = jnp.concatenate([own + item for item in bins], axis=1)
                inside = index >= offs_ref[1]
                real = jnp.where(inside, real, 0.0)
                imag = jnp.where(inside, imag, 0.0)
            out[window * share : (window + 1) * share, 2 * side] = real
            out[window * share : (window + 1) * share, 2 * side + 1] = imag


def range_focus(plan, sizes, count, offsets, first, second, tables):
    windows, share, bins = sizes
    lines_all = first.shape[1]
    lines = min(lines_all, SPAN)
    reach = max(SPAN * (windows - 1) - lead + depth for lead, depth in plan)
    block = pl.BlockSpec((2, lines, reach), lambda i: (0, i, 0))
    whole = pl.BlockSpec(memory_space=pltpu.VMEM)
    flops = sum(2 * 2 * lines_all * windows * depth * tables[0].shape[1] for _, depth in plan)
    return pl.pallas_call(
        functools.partial(range_kernel, plan, sizes),
        grid=(lines_all // lines,),
        out_shape=jax.ShapeDtypeStruct((count, 4, 8 * len(bins), lines_all), F32),
        in_specs=[pl.BlockSpec(memory_space=pltpu.SMEM), block, block, whole, whole],
        out_specs=pl.BlockSpec((count, 4, 8 * len(bins), lines), lambda i: (0, 0, 0, i)),
        compiler_params=pltpu.CompilerParams(vmem_limit_bytes=LIMIT),
        cost_estimate=pl.CostEstimate(flops=flops, bytes_accessed=16 << 20, transcendentals=0),
        name="ranges",
    )(offsets, first, second, *tables)


def azimuth_kernel(depth, group, offs_ref, got_ref, table, out, high, low, image):
    sources, _, bins, width = got_ref.shape
    spans = width // SPAN
    windows = sources * spans
    lines_all = windows * SPAN
    extra = high.shape[1] - windows
    cols = table.shape[1] // 2

    @pl.loop(0, sources)
    def _(source):
        for side in range(2):
            for part in range(spans):
                block = got_ref[
                    source, 2 * side : 2 * side + 2, :, part * SPAN : (part + 1) * SPAN
                ].reshape(2 * bins, SPAN)
                upper = block.astype(BF16)
                high[side, source * spans + part] = upper
                low[side, source * spans + part] = (block - upper.astype(F32)).astype(BF16)

    for side in range(2):
        for slot in range(extra):
            high[side, windows + slot] = high[side, slot % windows]
            low[side, windows + slot] = low[side, slot % windows]

    pads = jnp.zeros((4, bins, HALF), F32)
    image[:, :, 0:HALF] = pads
    image[:, :, HALF + lines_all :] = pads

    @pl.loop(0, 2 * (windows // group))
    def _(turn):
        side = turn // (windows // group)
        base = (turn % (windows // group)) * group

        def gathered(ref):
            pieces = []
            for unit in range(depth // SPAN):
                taken = ref[side, pl.ds(base + unit, group)]
                pieces.append(taken.reshape(group * 2 * bins, SPAN))
            return jnp.concatenate(pieces, axis=1)

        upper, lower = gathered(high), gathered(low)
        both = jnp.dot(upper, table[:, 0:cols], preferred_element_type=F32)
        both += jnp.dot(lower, table[:, 0:cols], preferred_element_type=F32)
        both += jnp.dot(upper, table[:, cols:], preferred_element_type=F32)
        both = both.reshape(group, 2, bins, cols)
        real = both[:, 0, :, 0:SPAN] + both[:, 1, :, SPAN:]
        imag = both[:, 1, :, 0:SPAN] - both[:, 0, :, SPAN:]
        for k in range(group):
            at = pl.ds(pl.multiple_of((base + k) * SPAN + HALF, HALF), SPAN)
            image[2 * side, :, at] = real[k]
            image[2 * side + 1, :, at] = imag[k]

    block = math.gcd(lines_all, 1024)
    length = block + 2 * HALF
    shift = jnp.where(offs_ref[0] < 0, offs_ref[0] + length, offs_ref[0])

    @pl.loop(0, lines_all // block)
    def _(step):
        start = pl.multiple_of(step * block, HALF)
        at = pl.ds(start, length)
        for row in range(0, bins, 8):
            rows = slice(row, row + 8)
            a, b = image[0, rows, at], image[1, rows, at]
            c = pltpu.roll(image[2, rows, at], shift, 1)
            d = pltpu.roll(image[3, rows, at], shift, 1)
            fields = (a * c + b * d, b * c - a * d, a * a + b * b, c * c + d * d)
            for k, value in enumerate(fields):
                line = lax.broadcasted_iota(jnp.int32, (8, length), 1) + (start - HALF)
                if k == 3:
                    value = jnp.where((line >= 0) & (line < lines_all), value, 0.0)
                for hop in (1, 2, 4):
                    value = value + pltpu.roll(value, length - hop, 1)
                out[k, rows, pl.ds(start, block)] = pltpu.roll(value, 3, 1)[:, HALF : HALF + block]


def azimuth_focus(depth, offsets, got, table):
    sources, _, bins, width = got.shape
    windows = sources * width // SPAN
    lines_all = windows * SPAN
    group = math.gcd(windows, max(1, 512 // (2 * bins)))
    vmem = pl.BlockSpec(memory_space=pltpu.VMEM)
    store = pltpu.VMEM((2, windows + depth // SPAN - 1, 2 * bins, SPAN), BF16)
    flops = 2 * 2 * 3 * windows * 2 * bins * depth * 2 * SPAN
    return pl.pallas_call(
        functools.partial(azimuth_kernel, depth, group),
        out_shape=jax.ShapeDtypeStruct((4, bins, lines_all), F32),
        in_specs=[pl.BlockSpec(memory_space=pltpu.SMEM)] + [vmem] * 2,
        out_specs=vmem,
        scratch_shapes=[store, store, pltpu.VMEM((4, bins, lines_all + 2 * HALF), F32)],
        compiler_params=pltpu.CompilerParams(vmem_limit_bytes=LIMIT),
        cost_estimate=pl.CostEstimate(flops=flops, bytes_accessed=8 << 20, transcendentals=0),
        name="azimuths",
    )(offsets, got, table)


def finish_kernel(layout, below_ref, above_ref, *refs):
    parts = refs[: len(layout)]
    picture, coherence, held = refs[len(layout) :]
    bins = coherence.shape[0]
    held[:, 0:3] = below_ref[:, 1:4]
    held[:, 3 + bins : 7 + bins] = above_ref[...]
    for part, starts in zip(parts, layout):
        for k, start in enumerate(starts):
            held[:, 3 + start : 11 + start] = part[:, 8 * k : 8 * k + 8]
    sums = []
    for field in range(4):
        total = held[field]
        for hop in (1, 2, 4):
            total = total + pltpu.roll(total, bins + 8 - hop, 0)
        sums.append(total[0:bins])
    picture[0] = sums[0] * (1.0 / 64.0)
    picture[1] = sums[1] * (1.0 / 64.0)
    coherence[...] = jnp.sqrt(sums[0] * sums[0] + sums[1] * sums[1]) / jnp.sqrt(sums[2] * sums[3] + 1.0)


def finish(layout, below, above, parts):
    lines_all = below.shape[2]
    bins = sum(part.shape[1] for part in parts)
    block = math.gcd(lines_all, 512)
    spec = lambda rows: pl.BlockSpec((4, rows, block), lambda i: (0, 0, i))
    return pl.pallas_call(
        functools.partial(finish_kernel, layout),
        grid=(lines_all // block,),
        out_shape=[
            jax.ShapeDtypeStruct((2, bins, lines_all), F32),
            jax.ShapeDtypeStruct((bins, lines_all), F32),
        ],
        in_specs=[spec(4), spec(4)] + [spec(part.shape[1]) for part in parts],
        out_specs=[
            pl.BlockSpec((2, bins, block), lambda i: (0, 0, i)),
            pl.BlockSpec((bins, block), lambda i: (0, i)),
        ],
        scratch_shapes=[pltpu.VMEM((4, bins + 8, block), F32)],
        compiler_params=pltpu.CompilerParams(vmem_limit_bytes=LIMIT),
        cost_estimate=pl.CostEstimate(flops=100 * bins * lines_all, bytes_accessed=16 << 20, transcendentals=0),
        name="finish",
    )(below, above, *parts)


def chunks_of(bins):
    if bins < 64:
        return [tuple(range(0, bins, 8))]
    inner = list(range(8, bins - 8, 8))
    return [(0, bins - 8), tuple(inner[:-2]), tuple(inner[-2:])]


def on_device(raw_first, raw_second, offsets, chirp_lengths):
    count = lax.axis_size("az")
    lines, range_count = raw_first.shape[1:]
    lines_all = lines * count
    reach = min(range_count, lines_all) // 4
    bins = WINDOW // count
    share = SPAN // bins
    plan = ((0, reach + SPAN), (HALF, reach + 2 * SPAN))
    real, imag = chirps(chirp_lengths, reach + 2 * SPAN)
    layout = chunks_of(bins)

    def columns(starts):
        return tuple(bins * k + start for k in range(share) for start in starts)

    def tables(row, starts, offset):
        return tuple((row, offset, lead, depth, starts) for lead, depth in plan)

    def turned(got):
        width = got.shape[3]
        if width % SPAN:
            fold = SPAN // width
            got = got.reshape(count // fold, fold, 4, got.shape[2], width)
            got = got.transpose(0, 2, 3, 1, 4).reshape(count // fold, 4, got.shape[3], SPAN)
        return got

    sizes = [(WINDOW // SPAN, share, starts) for starts in layout]
    along = tuple(8 * k for k in range(SPAN // 8))
    table_sets = [tables(0, columns(starts), 1) for starts in layout]
    table_sets[min(1, len(layout) - 1)] += tables(1, along, 0)[0:1]
    parts, given, azimuth_table = [], (offsets, real, imag), None
    exchanged = []
    for index, size in enumerate(sizes):
        made = make_tables(table_sets[index], *given)
        azimuth_table = made[2] if len(made) > 2 else azimuth_table
        sent = range_focus(plan, size, count, given[0], raw_first, raw_second, made[0:2])
        if exchanged:
            given, sent, exchanged[-1] = lax.optimization_barrier((given, sent, exchanged[-1]))
        else:
            given, sent = lax.optimization_barrier((given, sent))
        exchanged.append(lax.all_to_all(sent, "az", split_axis=0, concat_axis=0, tiled=True))
    for got in exchanged:
        parts.append(azimuth_focus(plan[0][1], offsets, turned(got), azimuth_table))
    up = [(i, i + 1) for i in range(count - 1)]
    down = [(j, i) for i, j in up]
    edge = parts[0]
    below = lax.ppermute(edge[:, edge.shape[1] - 4 :], "az", up)
    above = lax.ppermute(edge[:, 0:4], "az", down)
    return tuple(finish(layout, below, above, parts))


def solution(mesh):
    in_specs = (P("groups", "az", None), P("groups", "az", None), P("groups"), P("groups"))
    out_specs = (P("groups", "az", None), P(("groups", "az"), None))
    return jax.shard_map(
        on_device, mesh=mesh, in_specs=in_specs, out_specs=out_specs, check_vma=False
    )
```

time: 963 us -> 291 us (0.30)
  matrix products: 314 us -> 0 us
  other arithmetic: 315 us -> 4.48 us
  Pallas kernels: 0 us -> 214 us
  local copies, waits for them, and re-layouts: 166 us -> 3.07 us
  waiting for transfers between devices: 132 us -> 44.8 us
    dot_general x20 -> x0, matrix products: 314 us -> none  [complex_product(): jnp.einsum('c' + left_side + ',cd' + right_side + '->d' + result_side, st...]
    pallas_call x0 -> x10, Pallas kernels: none -> 214 us  [the longest x3 109 us: azimuth_focus(): pl.pallas_call(functools.partial(azimuth_kernel, depth, group), out_shape...]
    sub x6 -> x0, other arithmetic: 148 us -> none  [complex_times(): stacked[0] * other_real - stacked[1] * other_imag]
    another operation x11 -> x0, other arithmetic: 100 us -> none  [the longest x6 94.3 us: complex_times(): jnp.stack([stacked[0] * other_real - stacked[1] * other_imag, stacked[0]...]
    all_to_all x2 -> x3, waiting for transfers between devices: 120 us -> 44.8 us  [on_device(): lax.all_to_all(sent, 'az', split_axis=0, concat_axis=0, tiled=True)]
    another operation x2 -> x0, local copies, waits for them, and re-layouts: 64.5 us -> none  [complex_times(): jnp.stack([stacked[0] * other_real - stacked[1] * other_imag, stacked[0]...]
    add x3 -> x0, other arithmetic: 57.2 us -> none  [the longest x1 29.7 us: range_box(): result = result + extended[:, offset_bin:offset_bin + bins_count]]
    unnamed x46 -> x8, local copies, waits for them, and re-layouts: 30.3 us -> 2.89 us
  transfers between devices with their start and end apart: 4 -> 5, of which waited for: 4 -> 2; matrix products, arithmetic and copies ran while one was open for 6% -> 0% of each run, Pallas kernels for 0% -> 61%
where the time goes in v1:
time: 291 us; the launch traced here: 289 us
  Pallas kernels  214 us (74%)
  waiting for transfers between devices  44.8 us (15%)
  starting transfers between devices  22.3 us (8%)
  other arithmetic  4.48 us (2%)
  local copies, waits for them, and re-layouts  3.07 us (1%)
    pallas_call x3, Pallas kernels, azimuth_focus(): pl.pallas_call(functools.partial(azimuth_kernel, depth, group), out_shape...  109 us
    pallas_call x3, Pallas kernels, range_focus(): pl.pallas_call(functools.partial(range_kernel, plan, sizes), grid=(lines_...  57.8 us
    all_to_all x3, waiting for transfers between devices, on_device(): lax.all_to_all(sent, 'az', split_axis=0, concat_axis=0, tiled=True)  44.8 us
    pallas_call x3, Pallas kernels, make_tables(): pl.pallas_call(functools.partial(table_kernel, plan), out_shape=[jax.Shap...  33.4 us
    all_to_all x3, starting transfers between devices, on_device(): lax.all_to_all(sent, 'az', split_axis=0, concat_axis=0, tiled=True)  16.8 us
    pallas_call x1, Pallas kernels, finish(): pl.pallas_call(functools.partial(finish_kernel, layout), grid=(lines_all...  13.7 us
  transfers between devices with their start and end apart: 5, of which 2 were waited for; matrix products, arithmetic and copies ran while one was open for 0% of the time, Pallas kernels for 61%

profile of v1, /device:TPU:17, one launch (start us, length us, event | category | flops | bytes accessed | tf_op | source)
XLA Modules:
  0.0 289.3 jit_solution(4090902768867830520)
XLA Ops:
  0.6 0.7 compare_select_fusion.1
  1.3 0.7 broadcast_compare_fusion
  2.0 0.7 convert_rsqrt_fusion
  2.6 2.5 sine_multiply_fusion
  5.1 7.1 %tables.3 = (bf16[2304,256]{1,0:T(8,128)(2,1)}, bf16[2560,256]{1,0:T(8,128)(2,1)}) custom-call(s32[2]{0:T(128)} %offs_ref.13, f32[2,2560]{1,0:T(2,128)} %get-tuple-element.31.real_ref, f32[2,2560]{1,0:T(2,128)} %get-tuple-element.32.imag_ref), custom_call_target="tpu_custom_call" | custom-call | flops 249036800 | bytes 2490368 | tf_op jit(solution)/shard_map/tables/pallas_call | solution.py:65
  12.2 15.4 %ranges.3 = f32[16,4,16,512]{3,2,1,0:T(8,128)} custom-call(s32[2]{0:T(128)} %offs_ref.13, bf16[2,512,8192]{2,1,0:T(8,128)(2,1)} %first_ref.5, bf16[2,512,8192]{2,1,0:T(8,128)(2,1)} %second_ref.5, bf16[2304,256]{1,0:T(8,128)(2,1)} %get-tuple-element.20.refs_0_, bf16[2560,256]{1,0:T(8,128)(2,1)} %get-tuple-element.21.refs_1_), custom_call_target="tpu_custom_call" | custom-call | flops 10200547328 | bytes 16777216 | tf_op jit(solution)/shard_map/ranges/pallas_call | solution.py:122
  27.6 6.5 %all-to-all-start = ((f32[16,4,16,512]{3,2,1,0:T(8,128)}), f32[16,4,16,512]{3,2,1,0:T(8,128)S(1)}, u32[]{:S(2)}, u32[]{:S(2)}) async-start(f32[16,4,16,512]{3,2,1,0:T(8,128)} %ranges.3), calls=%async_computation | async-start | bytes 4194304 | tf_op jit(solution)/shard_map/all_to_all | solution.py:319
  34.1 19.1 %tables.4 = (bf16[2304,512]{1,0:T(8,128)(2,1)}, bf16[2560,512]{1,0:T(8,128)(2,1)}, bf16[2304,1024]{1,0:T(8,128)(2,1)}) custom-call(s32[2]{0:T(128)} %offs_ref.13, f32[2,2560]{1,0:T(2,128)} %get-tuple-element.31.real_ref, f32[2,2560]{1,0:T(2,128)} %get-tuple-element.32.imag_ref), custom_call_target="tpu_custom_call" | custom-call | flops 969932800 | bytes 9699328 | tf_op jit(solution)/shard_map/tables/pallas_call | solution.py:65
  53.2 27.0 %ranges.4 = f32[16,4,32,512]{3,2,1,0:T(8,128)} custom-call(s32[2]{0:T(128)} %offs_ref.13, bf16[2,512,8192]{2,1,0:T(8,128)(2,1)} %first_ref.5, bf16[2,512,8192]{2,1,0:T(8,128)(2,1)} %second_ref.5, bf16[2304,512]{1,0:T(8,128)(2,1)} %get-tuple-element.25.refs_0_, bf16[2560,512]{1,0:T(8,128)(2,1)} %get-tuple-element.26.refs_1_), custom_call_target="tpu_custom_call" | custom-call | flops 20401094656 | bytes 16777216 | tf_op jit(solution)/shard_map/ranges/pallas_call | solution.py:122
  80.2 1.0 all-to-all-done.got_ref
  81.1 0.0 copy-start.1
  81.1 1.3 copy-done.1
  82.5 5.2 %all-to-all-start.1 = ((f32[16,4,32,512]{3,2,1,0:T(8,128)}), f32[16,4,32,512]{3,2,1,0:T(8,128)}, u32[]{:S(2)}, u32[]{:S(2)}) async-start(f32[16,4,32,512]{3,2,1,0:T(8,128)} %ranges.4), calls=%async_computation.1 | async-start | bytes 8388608 | tf_op jit(solution)/shard_map/all_to_all | solution.py:319
  87.6 7.2 %tables.5 = (bf16[2304,256]{1,0:T(8,128)(2,1)}, bf16[2560,256]{1,0:T(8,128)(2,1)}) custom-call(s32[2]{0:T(128)} %offs_ref.13, f32[2,2560]{1,0:T(2,128)} %get-tuple-element.31.real_ref, f32[2,2560]{1,0:T(2,128)} %get-tuple-element.32.imag_ref), custom_call_target="tpu_custom_call" | custom-call | flops 249036800 | bytes 2490368 | tf_op jit(solution)/shard_map/tables/pallas_call | solution.py:65
  94.8 15.4 %ranges.5 = f32[16,4,16,512]{3,2,1,0:T(8,128)} custom-call(s32[2]{0:T(128)} %offs_ref.13, bf16[2,512,8192]{2,1,0:T(8,128)(2,1)} %first_ref.5, bf16[2,512,8192]{2,1,0:T(8,128)(2,1)} %second_ref.5, bf16[2304,256]{1,0:T(8,128)(2,1)} %get-tuple-element.33.refs_0_, bf16[2560,256]{1,0:T(8,128)(2,1)} %get-tuple-element.34.refs_1_), custom_call_target="tpu_custom_call" | custom-call | flops 10200547328 | bytes 16777216 | tf_op jit(solution)/shard_map/ranges/pallas_call | solution.py:122
  110.2 25.6 %azimuths.3.refs_0_ = f32[4,16,8192]{2,1,0:T(8,128)} custom-call(s32[2]{0:T(128)} %offs_ref.13, f32[16,4,16,512]{3,2,1,0:T(8,128)} %copy-done.1, bf16[2304,1024]{1,0:T(8,128)(2,1)} %get-tuple-element.29.table), custom_call_target="tpu_custom_call" | custom-call | flops 14495514624 | bytes 8388608 | tf_op jit(solution)/shard_map/azimuths/pallas_call | solution.py:217
  135.8 0.0 copy-start
  135.8 43.9 %all-to-all-done.1.got_ref = f32[16,4,32,512]{3,2,1,0:T(8,128)} async-done(((f32[16,4,32,512]{3,2,1,0:T(8,128)}), f32[16,4,32,512]{3,2,1,0:T(8,128)}, u32[]{:S(2)}, u32[]{:S(2)}) %all-to-all-start.1) | async-done | bytes 4194336 | tf_op jit(solution)/shard_map/all_to_all | solution.py:319
  179.7 5.2 %all-to-all-start.2 = ((f32[16,4,16,512]{3,2,1,0:T(8,128)}), f32[16,4,16,512]{3,2,1,0:T(8,128)}, u32[]{:S(2)}, u32[]{:S(2)}) async-start(f32[16,4,16,512]{3,2,1,0:T(8,128)} %ranges.5), calls=%async_computation.2 | async-start | bytes 4194304 | tf_op jit(solution)/shard_map/all_to_all | solution.py:319
  184.9 0.0 copy-done
  184.9 0.2 fusion.3
  185.1 3.4 %collective-permute-start = (f32[4,4,8192]{2,1,0:T(4,128)S(1)}, f32[4,4,8192]{2,1,0:T(4,128)S(1)}, u32[]{:S(2)}, u32[]{:S(2)}) collective-permute-start(f32[4,4,8192]{2,1,0:T(4,128)S(1)} %get-tuple-element.39), channel_id=1, source_target_pairs={{0,1},{1,2},{2,3},{3,4},{4,5},{5,6},{6,7},{7,8},{8,9},{9,10},{10,1... | collective-permute-start | bytes 1572872 | tf_op jit(solution)/shard_map/ppermute | solution.py:325
  188.4 2.2 collective-permute-start.1
  190.6 57.7 %azimuths.4.refs_1_ = f32[4,32,8192]{2,1,0:T(8,128)} custom-call(s32[2]{0:T(128)} %offs_ref.13, f32[16,4,32,512]{3,2,1,0:T(8,128)} %all-to-all-done.1.got_ref, bf16[2304,1024]{1,0:T(8,128)(2,1)} %get-tuple-element.29.table), custom_call_target="tpu_custom_call" | custom-call | flops 28991029248 | bytes 8388608 | tf_op jit(solution)/shard_map/azimuths/pallas_call | solution.py:217
  248.3 0.0 all-to-all-done.2.got_ref
  248.3 25.7 %azimuths.5.refs_2_ = f32[4,16,8192]{2,1,0:T(8,128)} custom-call(s32[2]{0:T(128)} %offs_ref.13, f32[16,4,16,512]{3,2,1,0:T(8,128)} %all-to-all-done.2.got_ref, bf16[2304,1024]{1,0:T(8,128)(2,1)} %get-tuple-element.29.table), custom_call_target="tpu_custom_call" | custom-call | flops 14495514624 | bytes 8388608 | tf_op jit(solution)/shard_map/azimuths/pallas_call | solution.py:217
  274.0 0.0 collective-permute-done.below_ref
  274.0 0.0 copy-start.2
  274.0 0.0 collective-permute-done.1.above_ref
  274.0 0.8 copy-done.2
  274.8 0.0 copy-start.3
  274.8 0.8 copy-done.3
  275.6 13.7 %finish.1 = (f32[2,64,8192]{2,1,0:T(8,128)}, f32[64,8192]{1,0:T(8,128)}) custom-call(f32[4,4,8192]{2,1,0:T(4,128)} %copy-done.2, f32[4,4,8192]{2,1,0:T(4,128)} %copy-done.3, f32[4,16,8192]{2,1,0:T(8,128)} %azimuths.3.refs_0_, f32[4,32,8192]{2,1,0:T(8,128)} %azimuths.4.refs_1_, f32[4,16,8192]{2,1,0:T(8,128)} %azimuths.5.refs_2_), custom_call_target="tpu_custom_call" | custom-call | flops 52428800 | bytes 16777216 | tf_op jit(solution)/shard_map/finish/pallas_call | solution.py:254
  (1 shorter events, 0.0 us)
Async XLA Ops:
  27.6 53.5 %all-to-all-start = ((f32[16,4,16,512]{3,2,1,0:T(8,128)}), f32[16,4,16,512]{3,2,1,0:T(8,128)S(1)}, u32[]{:S(2)}, u32[]{:S(2)}) async-start(f32[16,4,16,512]{3,2,1,0:T(8,128)} %ranges.3), calls=%async_computation | async-start | bytes 4194304 | tf_op jit(solution)/shard_map/all_to_all | solution.py:319
  81.1 1.3 copy-start.1
  82.5 97.2 %all-to-all-start.1 = ((f32[16,4,32,512]{3,2,1,0:T(8,128)}), f32[16,4,32,512]{3,2,1,0:T(8,128)}, u32[]{:S(2)}, u32[]{:S(2)}) async-start(f32[16,4,32,512]{3,2,1,0:T(8,128)} %ranges.4), calls=%async_computation.1 | async-start | bytes 8388608 | tf_op jit(solution)/shard_map/all_to_all | solution.py:319
  135.8 49.0 %copy-start = (f32[4,16,8192]{2,1,0:T(8,128)S(1)}, f32[4,16,8192]{2,1,0:T(8,128)}, u32[]{:S(2)}) copy-start(f32[4,16,8192]{2,1,0:T(8,128)} %azimuths.3.refs_0_) | copy-start | bytes 6291460
  179.7 68.6 %all-to-all-start.2 = ((f32[16,4,16,512]{3,2,1,0:T(8,128)}), f32[16,4,16,512]{3,2,1,0:T(8,128)}, u32[]{:S(2)}, u32[]{:S(2)}) async-start(f32[16,4,16,512]{3,2,1,0:T(8,128)} %ranges.5), calls=%async_computation.2 | async-start | bytes 4194304 | tf_op jit(solution)/shard_map/all_to_all | solution.py:319
  185.1 88.9 %collective-permute-start = (f32[4,4,8192]{2,1,0:T(4,128)S(1)}, f32[4,4,8192]{2,1,0:T(4,128)S(1)}, u32[]{:S(2)}, u32[]{:S(2)}) collective-permute-start(f32[4,4,8192]{2,1,0:T(4,128)S(1)} %get-tuple-element.39), channel_id=1, source_target_pairs={{0,1},{1,2},{2,3},{3,4},{4,5},{5,6},{6,7},{7,8},{8,9},{9,10},{10,1... | collective-permute-start | bytes 1572872 | tf_op jit(solution)/shard_map/ppermute | solution.py:325
  188.4 85.6 %collective-permute-start.1 = (f32[4,4,8192]{2,1,0:T(4,128)S(1)}, f32[4,4,8192]{2,1,0:T(4,128)S(1)}, u32[]{:S(2)}, u32[]{:S(2)}) collective-permute-start(f32[4,4,8192]{2,1,0:T(4,128)S(1)} %get-tuple-element.38), channel_id=1, source_target_pairs={{1,0},{2,1},{3,2},{4,3},{5,4},{6,5},{7,6},{8,7},{9,8},{10,9},{11,1... | collective-permute-start | bytes 1572872 | tf_op jit(solution)/shard_map/ppermute | solution.py:326
  274.0 0.8 copy-start.2
  274.8 0.8 copy-start.3

commit v2 on v1

v2 whole, which is shorter than its diff:
```python
import functools
import math

import jax
import jax.numpy as jnp
from jax import lax
from jax.experimental import pallas as pl
from jax.experimental.pallas import tpu as pltpu
from jax.sharding import PartitionSpec as P

WINDOW = 1024
MAXSHIFT = 16
SPAN = 256
HALF = 128
LIMIT = 60 * 1024 * 1024
ROOMY = 22 * 1024 * 1024

F32, BF16 = jnp.float32, jnp.bfloat16


def chirp_lines(length, depth):
    shape = (8, depth)
    sample = lax.broadcasted_iota(jnp.int32, shape, 1) - lax.broadcasted_iota(jnp.int32, shape, 0)
    held = (sample >= 0) & (sample < length)
    offset = jnp.where(held, 2 * sample - length, 0)
    square = offset * offset
    period = jnp.full(shape, 8 * length, jnp.int32)
    whole = (square.astype(F32) / period.astype(F32)).astype(jnp.int32)
    numerator = square - whole * period
    numerator = jnp.where(numerator < 0, numerator + period, numerator)
    numerator = jnp.where(numerator >= period, numerator - period, numerator)
    size = period.astype(F32) * 0.125
    angles = jnp.pi * numerator.astype(F32) / (4.0 * size)
    amplitude = jnp.where(held, 1.0 / jnp.sqrt(size), 0.0)
    return amplitude * jnp.cos(angles), amplitude * jnp.sin(angles)


def table_kernel(plan, offs_ref, lengths_ref, *refs):
    outs, scratch = refs[:-1], refs[-1]
    for (row, shifted, lead, depth, starts), out in zip(plan, outs):
        cols = 8 * len(starts)
        base = lead - offs_ref[1] if shifted else lead
        uniform = len(starts) > 8 and all(start == 8 * k for k, start in enumerate(starts))
        for part, line in enumerate(chirp_lines(lengths_ref[row], depth)):
            if uniform:
                held = line

                @pl.loop(0, len(starts))
                def _(k):
                    moved = pltpu.roll(held, base + 8 * k, 1)
                    scratch[pl.ds(pl.multiple_of(part * cols + 8 * k, 8), 8), 0:depth] = moved

            else:
                for k, start in enumerate(starts):
                    moved = pltpu.roll(line, base + start, 1)
                    scratch[part * cols + 8 * k : part * cols + 8 * k + 8, 0:depth] = moved

        @pl.loop(0, depth // HALF)
        def _(k):
            at = pl.ds(pl.multiple_of(k * HALF, HALF), HALF)
            turned = scratch[0 : 2 * cols, at].T
            if row:
                real, imag = turned[:, 0:cols], turned[:, cols:]
                turned = jnp.concatenate([real, real + imag, real - imag], axis=1)
            width = turned.shape[1]
            high = turned.astype(BF16)
            out[at, 0:width] = high
            out[at, width : 2 * width] = (turned - high.astype(F32)).astype(BF16)


def make_tables(plan, offsets, lengths):
    rows = max(2 * 8 * len(item[4]) for item in plan)
    depth = max(item[3] for item in plan)
    widths = [8 * len(item[4]) * (6 if item[0] else 4) for item in plan]
    size = sum(item[3] * width for item, width in zip(plan, widths))
    smem = pl.BlockSpec(memory_space=pltpu.SMEM)
    vmem = pl.BlockSpec(memory_space=pltpu.VMEM)
    return pl.pallas_call(
        functools.partial(table_kernel, plan),
        out_shape=[jax.ShapeDtypeStruct((item[3], width), BF16) for item, width in zip(plan, widths)],
        in_specs=[smem, smem],
        out_specs=[vmem] * len(plan),
        scratch_shapes=[pltpu.VMEM((rows, depth), F32)],
        compiler_params=pltpu.CompilerParams(vmem_limit_bytes=ROOMY if plan[0][0] else LIMIT),
        cost_estimate=pl.CostEstimate(flops=size * 400, bytes_accessed=2 * size, transcendentals=0),
        name="tables",
    )(offsets, lengths)


def range_kernel(plan, windows, share, groups, routes, looped, offs_ref, first_ref, second_ref, *refs):
    tables, outs = refs[0:2], refs[2:]
    lines = first_ref.shape[1]
    for side, (source, table) in enumerate(zip((first_ref, second_ref), tables)):
        lead, depth = plan[side]

        def run(window, source=source, table=table, side=side, lead=lead, depth=depth):
            still = isinstance(window, int)
            start = SPAN * window - lead
            if still and start < 0:
                empty = jnp.zeros((2 * lines, -start), BF16)
                inner = source[:, :, 0 : start + depth].reshape(2 * lines, start + depth)
                left = jnp.concatenate([empty, inner], axis=1)
            else:
                at = pl.ds(start if still else pl.multiple_of(start, HALF), depth)
                left = source[:, :, at].reshape(2 * lines, depth)
            for skip, eights in groups:
                cols = share * len(eights) * 8
                both = jnp.dot(left, table[skip : skip + depth], preferred_element_type=F32)
                turned = (both[:, 0 : 2 * cols] + both[:, 2 * cols :]).T
                real = turned[0:cols, 0:lines] + turned[cols:, lines:]
                imag = turned[0:cols, lines:] - turned[cols:, 0:lines]
                real = real.reshape(share, len(eights), 8, lines)
                imag = imag.reshape(share, len(eights), 8, lines)
                for k, eight in enumerate(eights):
                    pair = real[:, k], imag[:, k]
                    if side and still and window * SPAN + eight < MAXSHIFT:
                        shape = (share, 8, lines)
                        index = lax.broadcasted_iota(jnp.int32, shape, 0) * (SPAN // share)
                        index = index + lax.broadcasted_iota(jnp.int32, shape, 1)
                        inside = index + (window * SPAN + eight) >= offs_ref[1]
                        pair = [jnp.where(inside, value, 0.0) for value in pair]
                    chunk, slot = routes[eight]
                    for part, value in enumerate(pair):
                        place = pl.ds(window * share, share)
                        outs[chunk][place, 2 * side + part, 8 * slot : 8 * slot + 8] = value

        if looped:
            for window in range(side):
                run(window)
            pl.loop(side, windows)(run)
        else:
            for window in range(windows):
                run(window)


def range_focus(plan, share, groups, routes, looped, count, offsets, first, second, tables):
    windows = WINDOW // SPAN
    lines_all = first.shape[1]
    lines = min(lines_all, SPAN)
    reach = max(SPAN * (windows - 1) - lead + depth for lead, depth in plan)
    block = pl.BlockSpec((2, lines, reach), lambda i: (0, i, 0))
    whole = pl.BlockSpec(memory_space=pltpu.VMEM)
    sizes = [0] * (1 + max(chunk for chunk, _ in routes.values()))
    for chunk, _ in routes.values():
        sizes[chunk] += 8
    bins = sum(sizes)
    flops = sum(2 * 2 * lines_all * windows * depth * share * bins * 4 for _, depth in plan)
    return pl.pallas_call(
        functools.partial(range_kernel, plan, windows, share, groups, routes, looped),
        grid=(lines_all // lines,),
        out_shape=[jax.ShapeDtypeStruct((count, 4, size, lines_all), F32) for size in sizes],
        in_specs=[pl.BlockSpec(memory_space=pltpu.SMEM), block, block, whole, whole],
        out_specs=[pl.BlockSpec((count, 4, size, lines), lambda i: (0, 0, 0, i)) for size in sizes],
        compiler_params=pltpu.CompilerParams(vmem_limit_bytes=LIMIT),
        cost_estimate=pl.CostEstimate(flops=flops, bytes_accessed=16 << 20, transcendentals=0),
        name="ranges",
    )(offsets, first, second, *tables)


def azimuth_kernel(depth, group, offs_ref, got_ref, table, out, high, low, image):
    sources, _, bins, width = got_ref.shape
    spans = width // SPAN
    windows = sources * spans
    lines_all = windows * SPAN
    extra = high.shape[1] - windows
    rows = 2 * bins

    @pl.loop(0, sources)
    def _(source):
        for part in range(spans):
            at = slice(part * SPAN, (part + 1) * SPAN)
            real = jnp.concatenate([got_ref[source, 0, :, at], got_ref[source, 2, :, at]], axis=0)
            imag = jnp.concatenate([got_ref[source, 1, :, at], got_ref[source, 3, :, at]], axis=0)
            for kind, value in enumerate((real + imag, real, imag)):
                upper = value.astype(BF16)
                high[kind, source * spans + part] = upper
                low[kind, source * spans + part] = (value - upper.astype(F32)).astype(BF16)

    for kind in range(3):
        for slot in range(extra):
            high[kind, windows + slot] = high[kind, slot % windows]
            low[kind, windows + slot] = low[kind, slot % windows]

    pads = jnp.zeros((4, bins, HALF), F32)
    image[:, :, 0:HALF] = pads
    image[:, :, HALF + lines_all :] = pads

    @pl.loop(0, windows // group)
    def _(turn):
        base = turn * group

        def gathered(ref, kind):
            pieces = []
            for unit in range(depth // SPAN):
                taken = ref[kind, pl.ds(base + unit, group)]
                pieces.append(taken.reshape(group * rows, SPAN))
            return jnp.concatenate(pieces, axis=1)

        products = []
        for kind in range(3):
            upper, lower = gathered(high, kind), gathered(low, kind)
            near = table[:, kind * SPAN : (kind + 1) * SPAN]
            far = table[:, (3 + kind) * SPAN : (4 + kind) * SPAN]
            both = jnp.dot(upper, near, preferred_element_type=F32)
            both += jnp.dot(lower, near, preferred_element_type=F32)
            both += jnp.dot(upper, far, preferred_element_type=F32)
            products.append(both)
        real = (products[0] - products[2]).reshape(group, 2, bins, SPAN)
        imag = (products[0] - products[1]).reshape(group, 2, bins, SPAN)
        for k in range(group):
            at = pl.ds(pl.multiple_of((base + k) * SPAN + HALF, HALF), SPAN)
            for side in range(2):
                image[2 * side, :, at] = real[k, side]
                image[2 * side + 1, :, at] = imag[k, side]

    block = math.gcd(lines_all, 1024)
    length = block + 2 * HALF
    shift = jnp.where(offs_ref[0] < 0, offs_ref[0] + length, offs_ref[0])

    @pl.loop(0, lines_all // block)
    def _(step):
        start = pl.multiple_of(step * block, HALF)
        at = pl.ds(start, length)
        for row in range(0, bins, 8):
            here = slice(row, row + 8)
            a, b = image[0, here, at], image[1, here, at]
            c = pltpu.roll(image[2, here, at], shift, 1)
            d = pltpu.roll(image[3, here, at], shift, 1)
            fields = (a * c + b * d, b * c - a * d, a * a + b * b, c * c + d * d)
            for k, value in enumerate(fields):
                line = lax.broadcasted_iota(jnp.int32, (8, length), 1) + (start - HALF)
                if k == 3:
                    value = jnp.where((line >= 0) & (line < lines_all), value, 0.0)
                for hop in (1, 2, length - 4):
                    value = value + pltpu.roll(value, hop, 1)
                out[k, here, pl.ds(start, block)] = value[:, HALF : HALF + block]


def azimuth_focus(depth, offsets, got, table):
    sources, _, bins, width = got.shape
    windows = sources * width // SPAN
    lines_all = windows * SPAN
    group = math.gcd(windows, 32)
    smem, vmem = pl.BlockSpec(memory_space=pltpu.SMEM), pl.BlockSpec(memory_space=pltpu.VMEM)
    block = pl.BlockSpec((sources, 4, 8, width), lambda i: (0, 0, i, 0))
    store = pltpu.VMEM((3, windows + depth // SPAN - 1, 16, SPAN), BF16)
    flops = 2 * 3 * 3 * windows * 2 * bins * depth * SPAN
    return pl.pallas_call(
        functools.partial(azimuth_kernel, depth, group),
        out_shape=jax.ShapeDtypeStruct((4, bins, lines_all), F32),
        grid=(bins // 8,),
        in_specs=[smem, block, vmem],
        out_specs=pl.BlockSpec((4, 8, lines_all), lambda i: (0, i, 0)),
        scratch_shapes=[
            store,
            store,
            pltpu.VMEM((4, 8, lines_all + 2 * HALF), F32),
        ],
        compiler_params=pltpu.CompilerParams(vmem_limit_bytes=ROOMY),
        cost_estimate=pl.CostEstimate(flops=flops, bytes_accessed=8 << 20, transcendentals=0),
        name="azimuths",
    )(offsets, got, table)


def finish_kernel(bins, start, eights, below_ref, above_ref, *refs):
    *parts, picture, coherence, held = refs
    size = coherence.shape[0]
    held[:, 4:8] = below_ref[...]
    held[:, 8 + bins : 12 + bins] = above_ref[...]
    for eight, part in zip(eights, parts):
        held[:, 8 + eight : 16 + eight] = part[...]
    sums = []
    for field in range(4):
        total = held[field, start : start + size + 16]
        for hop in (1, 2, size + 12):
            total = total + pltpu.roll(total, hop, 0)
        sums.append(total[8 : 8 + size])
    picture[0] = sums[0] * (1.0 / 64.0)
    picture[1] = sums[1] * (1.0 / 64.0)
    strength = jnp.sqrt(sums[0] * sums[0] + sums[1] * sums[1])
    coherence[...] = strength / jnp.sqrt(sums[2] * sums[3] + 1.0)


def finish(bins, start, size, parts, routes, borders, before=()):
    lines_all = parts[0].shape[2]
    block = math.gcd(lines_all, 2048)
    every = range(max(0, (start - 3) // 8), min(bins // 8, (start + size + 3) // 8 + 1))
    eights = [8 * k for k in every]
    operands, specs = list(borders), [pl.BlockSpec((4, 4, block), lambda i: (0, 0, i))] * 2
    for eight in eights:
        chunk, slot = routes[eight]
        operands.append(parts[chunk])
        specs.append(pl.BlockSpec((4, 8, block), lambda i, slot=slot: (0, slot, i)))
    index = start // size
    given = len(operands)

    def kernel(*refs):
        finish_kernel(bins, start, eights, *refs[:given], *refs[given + len(before) :])

    return pl.pallas_call(
        kernel,
        grid=(lines_all // block,),
        out_shape=[
            jax.ShapeDtypeStruct((2, bins, lines_all), F32),
            jax.ShapeDtypeStruct((bins, lines_all), F32),
        ],
        in_specs=specs + [pl.BlockSpec(memory_space=pl.ANY)] * len(before),
        out_specs=[
            pl.BlockSpec((2, size, block), lambda i: (0, index, i)),
            pl.BlockSpec((size, block), lambda i: (index, i)),
        ],
        scratch_shapes=[pltpu.VMEM((4, bins + 16, block), F32)],
        input_output_aliases={given: 0, given + 1: 1} if before else {},
        compiler_params=pltpu.CompilerParams(vmem_limit_bytes=ROOMY),
        cost_estimate=pl.CostEstimate(
            flops=3000 * size * lines_all, bytes_accessed=16 << 20, transcendentals=0
        ),
        name="finish",
    )(*operands, *before)


def arrangement(bins):
    if bins < 64:
        every = tuple(range(0, bins, 8))
        return [every], [[(0, every)]]
    chunks = [(0, bins - 8), (8, 16, 24, 32), (40, 48)]
    return chunks, [[(0, (0, bins - 8))], [(8, (8, 16)), (8, (24, 32))], [(8, (40, 48))]]


def on_device(raw_first, raw_second, offsets, chirp_lengths):
    count = lax.axis_size("az")
    lines, range_count = raw_first.shape[1:]
    lines_all = lines * count
    reach = min(range_count, lines_all) // 4
    bins = WINDOW // count
    share = SPAN // bins
    plan = ((0, reach + SPAN), (HALF, reach + 2 * SPAN))
    chunks, calls = arrangement(bins)
    routes = {eight: (k, slot) for k, chunk in enumerate(chunks) for slot, eight in enumerate(chunk)}

    def columns(starts):
        return tuple(bins * k + start for k in range(share) for start in starts)

    def pair(starts, spare):
        return tuple(
            (0, side, lead + spare, depth + spare, columns(starts))
            for side, (lead, depth) in enumerate(plan)
        )

    def turned(got):
        width = got.shape[3]
        if width % SPAN:
            fold = SPAN // width
            got = got.reshape(count // fold, fold, 4, got.shape[2], width)
            got = got.transpose(0, 2, 3, 1, 4).reshape(count // fold, 4, got.shape[3], SPAN)
        return got

    along = ((1, 0, 0, plan[0][1], tuple(8 * k for k in range(SPAN // 8))),)
    head = make_tables(pair(chunks[0], 0), offsets, chirp_lengths)
    sent, given, ready = {}, offsets, head
    exchanged = []
    for index, call in enumerate(calls):
        if index == 1:
            ready = make_tables(pair(call[0][1], HALF), given, chirp_lengths)
        spare = HALF if index else 0
        groups = [(spare - (eights[0] - start) if index else 0, eights) for start, eights in call]
        local = {}
        owners = sorted({routes[eight][0] for _, eights in call for eight in eights})
        for _, eights in call:
            for eight in eights:
                chunk, slot = routes[eight]
                local[eight] = (owners.index(chunk), slot)
        results = range_focus(
            plan, share, groups, local, index > 1, count, given, raw_first, raw_second, ready
        )
        for owner, result in zip(owners, results):
            sent[owner] = result
        given, sent[owners[0]] = lax.optimization_barrier((given, sent[owners[0]]))
        if index < 2:
            exchanged.append(exchange(sent[index], exchanged))
        if index == 0:
            continue
        if index == 1:
            given = lax.optimization_barrier((given, exchanged[0]))[0]
    base = make_tables(along, given, chirp_lengths)[0]
    up = [(i, i + 1) for i in range(count - 1)]
    down = [(j, i) for i, j in up]
    parts, borders = [], None
    for index in range(len(chunks)):
        if index >= len(exchanged):
            earlier = (parts[index - 2], borders) if index > 1 else (given, borders)
            sent[index], earlier = lax.optimization_barrier((sent[index], earlier))
            if index > 1:
                parts[index - 2], borders = earlier
            exchanged.append(exchange(sent[index], exchanged))
        if index:
            parts.append(azimuth_focus(plan[0][1], offsets, turned(exchanged[index - 1]), base))
        if index == 1:
            borders = bordering(parts[0], up, down)
    parts.append(azimuth_focus(plan[0][1], offsets, turned(exchanged[-1]), base))
    if len(chunks) == 1:
        borders = bordering(parts[0], up, down)
        return tuple(finish(bins, 0, bins, parts, routes, borders))
    outs = finish(bins, 0, bins // 2, parts, routes, borders)
    return tuple(finish(bins, bins // 2, bins // 2, parts, routes, borders, tuple(outs)))


def bordering(part, up, down):
    below = lax.ppermute(part[:, part.shape[1] - 4 :], "az", up)
    return below, lax.ppermute(part[:, 0:4], "az", down)


def exchange(value, earlier):
    if earlier:
        value, earlier[-1] = lax.optimization_barrier((value, earlier[-1]))
    return lax.all_to_all(value, "az", split_axis=0, concat_axis=0, tiled=True)


def solution(mesh):
    in_specs = (P("groups", "az", None), P("groups", "az", None), P("groups"), P("groups"))
    out_specs = (P("groups", "az", None), P(("groups", "az"), None))
    return jax.shard_map(
        on_device, mesh=mesh, in_specs=in_specs, out_specs=out_specs, check_vma=False
    )
```

time: 291 us -> 262 us (0.900)
  Pallas kernels: 214 us -> 170 us
  waiting for transfers between devices: 44.8 us -> 52.7 us
  local copies, waits for them, and re-layouts: 3.07 us -> 9.62 us
  starting transfers between devices: 22.3 us -> 27.5 us
  other arithmetic: 4.48 us -> 0 us
    pallas_call x3, Pallas kernels: 109 us -> 73.6 us  [azimuth_focus(): pl.pallas_call(functools.partial(azimuth_kernel, depth, group), out_shape...]
    ppermute x2, waiting for transfers between devices: 0.01 us -> 11 us  [the longest x1 11 us: bordering(): return (below, lax.ppermute(part[:, 0:4], 'az', down))]
    pallas_call x3, Pallas kernels: 33.4 us -> 25 us  [make_tables(): pl.pallas_call(functools.partial(table_kernel, plan), out_shape=[jax.Shap...]
    unnamed x8 -> x18, local copies, waits for them, and re-layouts: 2.89 us -> 9.44 us
    all_to_all x3, starting transfers between devices: 16.8 us -> 21.9 us  [exchange(): return lax.all_to_all(value, 'az', split_axis=0, concat_axis=0, tiled=True)]
    all_to_all x3, waiting for transfers between devices: 44.8 us -> 41.7 us  [exchange(): return lax.all_to_all(value, 'az', split_axis=0, concat_axis=0, tiled=True)]
    pallas_call x4 -> x5, Pallas kernels: 71.5 us -> 71.5 us  [the longest x3 60.4 us: range_focus(): pl.pallas_call(functools.partial(range_kernel, plan, windows, share, grou...]
  transfers between devices with their start and end apart: 5 -> 5, of which waited for: 2 -> 4; matrix products, arithmetic and copies ran while one was open for 0% -> 0% of each run, Pallas kernels for 61% -> 47%
where the time goes in v2:
time: 262 us; the launch traced here: 261 us
  Pallas kernels  170 us (65%)
  waiting for transfers between devices  52.7 us (20%)
  starting transfers between devices  27.5 us (10%)
  local copies, waits for them, and re-layouts  9.62 us (4%)
    pallas_call x3, Pallas kernels, azimuth_focus(): pl.pallas_call(functools.partial(azimuth_kernel, depth, group), out_shape...  73.6 us
    pallas_call x3, Pallas kernels, range_focus(): pl.pallas_call(functools.partial(range_kernel, plan, windows, share, grou...  60.4 us
    all_to_all x3, waiting for transfers between devices, exchange(): return lax.all_to_all(value, 'az', split_axis=0, concat_axis=0, tiled=True)  41.7 us
    pallas_call x3, Pallas kernels, make_tables(): pl.pallas_call(functools.partial(table_kernel, plan), out_shape=[jax.Shap...  25 us
    all_to_all x3, starting transfers between devices, exchange(): return lax.all_to_all(value, 'az', split_axis=0, concat_axis=0, tiled=True)  21.9 us
    pallas_call x2, Pallas kernels, finish(): pl.pallas_call(kernel, grid=(lines_all // block,), out_shape=[jax.ShapeDt...  11.1 us
    ppermute x1, waiting for transfers between devices, bordering(): return (below, lax.ppermute(part[:, 0:4], 'az', down))  11 us
    unnamed x18, local copies, waits for them, and re-layouts  9.44 us
  transfers between devices with their start and end apart: 5, of which 4 were waited for; matrix products, arithmetic and copies ran while one was open for 0% of the time, Pallas kernels for 47%

profile of v2, /device:TPU:17, one launch (start us, length us, event | category | flops | bytes accessed | tf_op | source)
XLA Modules:
  0.0 260.7 jit_solution(17884249344100939125)
XLA Ops:
  0.6 7.4 %tables.3 = (bf16[2304,256]{1,0:T(8,128)(2,1)}, bf16[2560,256]{1,0:T(8,128)(2,1)}) custom-call(s32[2]{0:T(128)} %offs_ref.13, s32[2]{0:T(128)} %lengths_ref.5), custom_call_target="tpu_custom_call" | custom-call | flops 498073600 | bytes 2490368 | tf_op jit(solution)/shard_map/tables/pallas_call | solution.py:78
  8.0 15.4 %ranges.3 = f32[16,4,16,512]{3,2,1,0:T(8,128)} custom-call(s32[2]{0:T(128)} %offs_ref.13, bf16[2,512,8192]{2,1,0:T(8,128)(2,1)} %first_ref.5, bf16[2,512,8192]{2,1,0:T(8,128)(2,1)} %second_ref.5, bf16[2304,256]{1,0:T(8,128)(2,1)} %get-tuple-element.23.refs_0_, bf16[2560,256]{1,0:T(8,128)(2,1)} %get-tuple-element.24.refs_1_), custom_call_target="tpu_custom_call" | custom-call | flops 10200547328 | bytes 16777216 | tf_op jit(solution)/shard_map/ranges/pallas_call | solution.py:148
  23.4 6.5 %all-to-all-start = ((f32[16,4,16,512]{3,2,1,0:T(8,128)}), f32[16,4,16,512]{3,2,1,0:T(8,128)S(1)}, u32[]{:S(2)}, u32[]{:S(2)}) async-start(f32[16,4,16,512]{3,2,1,0:T(8,128)} %ranges.3), calls=%async_computation | async-start | bytes 4194304 | tf_op jit(solution)/shard_map/all_to_all | solution.py:416
  29.9 7.8 %tables.4 = (bf16[2432,256]{1,0:T(8,128)(2,1)}, bf16[2688,256]{1,0:T(8,128)(2,1)}) custom-call(s32[2]{0:T(128)} %offs_ref.13, s32[2]{0:T(128)} %lengths_ref.5), custom_call_target="tpu_custom_call" | custom-call | flops 524288000 | bytes 2621440 | tf_op jit(solution)/shard_map/tables/pallas_call | solution.py:78
  37.7 26.1 %ranges.4 = f32[16,4,32,512]{3,2,1,0:T(8,128)} custom-call(s32[2]{0:T(128)} %offs_ref.13, bf16[2,512,8192]{2,1,0:T(8,128)(2,1)} %first_ref.5, bf16[2,512,8192]{2,1,0:T(8,128)(2,1)} %second_ref.5, bf16[2432,256]{1,0:T(8,128)(2,1)} %get-tuple-element.26.refs_0_, bf16[2688,256]{1,0:T(8,128)(2,1)} %get-tuple-element.27.refs_1_), custom_call_target="tpu_custom_call" | custom-call | flops 20401094656 | bytes 16777216 | tf_op jit(solution)/shard_map/ranges/pallas_call | solution.py:148
  63.7 13.2 %all-to-all-done.got_ref = f32[16,4,16,512]{3,2,1,0:T(8,128)S(1)} async-done(((f32[16,4,16,512]{3,2,1,0:T(8,128)}), f32[16,4,16,512]{3,2,1,0:T(8,128)S(1)}, u32[]{:S(2)}, u32[]{:S(2)}) %all-to-all-start) | async-done | bytes 2097184 | tf_op jit(solution)/shard_map/all_to_all | solution.py:416
  76.9 0.0 copy-start.5
  77.0 1.3 copy-done.5
  78.3 5.2 %all-to-all-start.1 = ((f32[16,4,32,512]{3,2,1,0:T(8,128)}), f32[16,4,32,512]{3,2,1,0:T(8,128)}, u32[]{:S(2)}, u32[]{:S(2)}) async-start(f32[16,4,32,512]{3,2,1,0:T(8,128)} %ranges.4), calls=%async_computation.1 | async-start | bytes 8388608 | tf_op jit(solution)/shard_map/all_to_all | solution.py:416
  83.4 0.0 copy-start.7
  83.4 0.0 copy-start.8
  83.4 18.9 %ranges.5 = f32[16,4,16,512]{3,2,1,0:T(8,128)} custom-call(s32[2]{0:T(128)} %offs_ref.13, bf16[2,512,8192]{2,1,0:T(8,128)(2,1)} %first_ref.5, bf16[2,512,8192]{2,1,0:T(8,128)(2,1)} %second_ref.5, bf16[2432,256]{1,0:T(8,128)(2,1)} %get-tuple-element.26.refs_0_, bf16[2688,256]{1,0:T(8,128)(2,1)} %get-tuple-element.27.refs_1_), custom_call_target="tpu_custom_call" | custom-call | flops 10200547328 | bytes 16777216 | tf_op jit(solution)/shard_map/ranges/pallas_call | solution.py:148
  102.4 0.0 copy-done.7
  102.4 0.0 copy-done.8
  102.4 0.0 copy-start.6
  102.4 9.8 %tables.5.table = bf16[2304,1536]{1,0:T(8,128)(2,1)S(1)} custom-call(s32[2]{0:T(128)S(1)} %copy-done.7, s32[2]{0:T(128)S(1)} %copy-done.8), custom_call_target="tpu_custom_call" | custom-call | flops 1415577600 | bytes 7077888 | tf_op jit(solution)/shard_map/tables/pallas_call | solution.py:78
  112.2 0.0 copy-done.6
  112.2 0.0 copy-start.2
  112.2 18.2 %azimuths.3.refs_2_.refs_6_ = f32[4,16,8192]{2,1,0:T(8,128)S(1)} custom-call(s32[2]{0:T(128)S(1)} %copy-done.7, f32[16,4,16,512]{3,2,1,0:T(8,128)S(1)} %copy-done.6, bf16[2304,1536]{1,0:T(8,128)(2,1)S(1)} %tables.5.table), custom_call_target="tpu_custom_call" | custom-call | flops 10871635968 | bytes 8388608 | tf_op jit(solution)/shard_map/azimuths/pallas_call | solution.py:248
  130.4 0.0 copy-done.2
  130.5 0.2 fusion
  130.6 2.4 collective-permute-start.1
  133.0 3.2 %collective-permute-start = (f32[4,4,8192]{2,1,0:T(4,128)S(1)}, f32[4,4,8192]{2,1,0:T(4,128)S(1)}, u32[]{:S(2)}, u32[]{:S(2)}) collective-permute-start(f32[4,4,8192]{2,1,0:T(4,128)S(1)} %get-tuple-element.45), channel_id=1, source_target_pairs={{0,1},{1,2},{2,3},{3,4},{4,5},{5,6},{6,7},{7,8},{8,9},{9,10},{10,1... | collective-permute-start | bytes 1572872 | tf_op jit(solution)/shard_map/ppermute | solution.py:409
  136.2 11.0 %collective-permute-done.1.refs_1_ = f32[4,4,8192]{2,1,0:T(4,128)S(1)} collective-permute-done((f32[4,4,8192]{2,1,0:T(4,128)S(1)}, f32[4,4,8192]{2,1,0:T(4,128)S(1)}, u32[]{:S(2)}, u32[]{:S(2)}) %collective-permute-start.1) | collective-permute-done | bytes 524320 | tf_op jit(solution)/shard_map/ppermute | solution.py:410
  147.3 0.0 collective-permute-done.refs_0_
  147.3 28.3 %all-to-all-done.1.got_ref = f32[16,4,32,512]{3,2,1,0:T(8,128)} async-done(((f32[16,4,32,512]{3,2,1,0:T(8,128)}), f32[16,4,32,512]{3,2,1,0:T(8,128)}, u32[]{:S(2)}, u32[]{:S(2)}) %all-to-all-start.1) | async-done | bytes 4194336 | tf_op jit(solution)/shard_map/all_to_all | solution.py:416
  175.5 10.3 %all-to-all-start.2 = ((f32[16,4,16,512]{3,2,1,0:T(8,128)}), f32[16,4,16,512]{3,2,1,0:T(8,128)}, u32[]{:S(2)}, u32[]{:S(2)}) async-start(f32[16,4,16,512]{3,2,1,0:T(8,128)} %ranges.5), calls=%async_computation.2 | async-start | bytes 4194304 | tf_op jit(solution)/shard_map/all_to_all | solution.py:416
  185.8 0.0 copy-start.3
  185.8 3.0 %copy-done.3 = bf16[2304,1536]{1,0:T(8,128)(2,1)S(1)} copy-done((bf16[2304,1536]{1,0:T(8,128)(2,1)S(1)}, bf16[2304,1536]{1,0:T(8,128)(2,1)}, u32[]{:S(2)}) %copy-start.3) | copy-done | bytes 7077912
  188.8 36.4 %azimuths.4.refs_3_.refs_4_.refs_5_.refs_6_.refs_2_ = f32[4,32,8192]{2,1,0:T(8,128)S(1)} custom-call(s32[2]{0:T(128)S(1)} %copy-done.7, f32[16,4,32,512]{3,2,1,0:T(8,128)} %all-to-all-done.1.got_ref, bf16[2304,1536]{1,0:T(8,128)(2,1)S(1)} %copy-done.3), custom_call_target="tpu_custom_call" | custom-call | flops 21743271936 | bytes 8388608 | tf_op jit(solution)/shard_map/azimuths/pallas_call | solution.py:248
  225.3 5.5 %finish.2 = (f32[2,64,8192]{2,1,0:T(8,128)}, f32[64,8192]{1,0:T(8,128)}) custom-call(f32[4,4,8192]{2,1,0:T(4,128)S(1)} %collective-permute-done.refs_0_, f32[4,4,8192]{2,1,0:T(4,128)S(1)} %collective-permute-done.1.refs_1_, f32[4,16,8192]{2,1,0:T(8,128)S(1)} %azimuths.3.refs_2_.refs_6_, f32[4,32,8192]{2,1,0:T(8,128)S(1)} %azimuths.4.refs_3_.refs_4_.refs_5_.refs_6_.refs_2_, ...), custom_call_target="tpu_custom_call" | custom-call | flops 786432000 | bytes 16777216 | tf_op jit(solution)/shard_map/finish/pallas_call | solution.py:300
  230.8 0.0 copy-start
  230.8 2.1 copy-done
  232.9 0.2 all-to-all-done.2.got_ref
  233.1 0.0 copy-start.4
  233.1 3.0 %copy-done.4 = bf16[2304,1536]{1,0:T(8,128)(2,1)S(1)} copy-done((bf16[2304,1536]{1,0:T(8,128)(2,1)S(1)}, bf16[2304,1536]{1,0:T(8,128)(2,1)}, u32[]{:S(2)}) %copy-start.4) | copy-done | bytes 7077912
  236.1 0.0 copy-start.1
  236.1 19.0 %azimuths.5.refs_4_.refs_5_ = f32[4,16,8192]{2,1,0:T(8,128)S(1)} custom-call(s32[2]{0:T(128)S(1)} %copy-done.7, f32[16,4,16,512]{3,2,1,0:T(8,128)} %all-to-all-done.2.got_ref, bf16[2304,1536]{1,0:T(8,128)(2,1)S(1)} %copy-done.4), custom_call_target="tpu_custom_call" | custom-call | flops 10871635968 | bytes 8388608 | tf_op jit(solution)/shard_map/azimuths/pallas_call | solution.py:248
  255.1 0.0 copy-done.1
  255.1 5.6 %finish.3 = (f32[2,64,8192]{2,1,0:T(8,128)}, f32[64,8192]{1,0:T(8,128)}) custom-call(f32[4,4,8192]{2,1,0:T(4,128)S(1)} %collective-permute-done.refs_0_, f32[4,4,8192]{2,1,0:T(4,128)S(1)} %collective-permute-done.1.refs_1_, f32[4,32,8192]{2,1,0:T(8,128)S(1)} %copy-done.1, ...), custom_call_target="tpu_custom_call", output_to_operand_aliasing={{0}: (7, {}), {1}: (8, {})} | custom-call | flops 786432000 | bytes 16777216 | tf_op jit(solution)/shard_map/finish/pallas_call | solution.py:300
Async XLA Ops:
  23.4 53.5 %all-to-all-start = ((f32[16,4,16,512]{3,2,1,0:T(8,128)}), f32[16,4,16,512]{3,2,1,0:T(8,128)S(1)}, u32[]{:S(2)}, u32[]{:S(2)}) async-start(f32[16,4,16,512]{3,2,1,0:T(8,128)} %ranges.3), calls=%async_computation | async-start | bytes 4194304 | tf_op jit(solution)/shard_map/all_to_all | solution.py:416
  76.9 1.3 copy-start.5
  78.3 97.2 %all-to-all-start.1 = ((f32[16,4,32,512]{3,2,1,0:T(8,128)}), f32[16,4,32,512]{3,2,1,0:T(8,128)}, u32[]{:S(2)}, u32[]{:S(2)}) async-start(f32[16,4,32,512]{3,2,1,0:T(8,128)} %ranges.4), calls=%async_computation.1 | async-start | bytes 8388608 | tf_op jit(solution)/shard_map/all_to_all | solution.py:416
  83.4 19.0 %copy-start.7 = (s32[2]{0:T(128)S(1)}, s32[2]{0:T(128)}, u32[]{:S(2)}) copy-start(s32[2]{0:T(128)} %offs_ref.13) | copy-start | bytes 28
  83.4 19.0 %copy-start.8 = (s32[2]{0:T(128)S(1)}, s32[2]{0:T(128)}, u32[]{:S(2)}) copy-start(s32[2]{0:T(128)} %lengths_ref.5) | copy-start | bytes 28
  102.4 9.8 %copy-start.6 = (f32[16,4,16,512]{3,2,1,0:T(8,128)S(1)}, f32[16,4,16,512]{3,2,1,0:T(8,128)}, u32[]{:S(2)}) copy-start(f32[16,4,16,512]{3,2,1,0:T(8,128)} %copy-done.5) | copy-start | bytes 6291460
  112.2 18.3 %copy-start.2 = (bf16[2304,1536]{1,0:T(8,128)(2,1)}, bf16[2304,1536]{1,0:T(8,128)(2,1)S(1)}, u32[]{:S(2)}) copy-start(bf16[2304,1536]{1,0:T(8,128)(2,1)S(1)} %tables.5.table) | copy-start | bytes 21233668
  130.6 16.6 %collective-permute-start.1 = (f32[4,4,8192]{2,1,0:T(4,128)S(1)}, f32[4,4,8192]{2,1,0:T(4,128)S(1)}, u32[]{:S(2)}, u32[]{:S(2)}) collective-permute-start(f32[4,4,8192]{2,1,0:T(4,128)S(1)} %get-tuple-element.44), channel_id=1, source_target_pairs={{1,0},{2,1},{3,2},{4,3},{5,4},{6,5},{7,6},{8,7},{9,8},{10,9},{11,1... | collective-permute-start | bytes 1572872 | tf_op jit(solution)/shard_map/ppermute | solution.py:410
  133.0 14.2 %collective-permute-start = (f32[4,4,8192]{2,1,0:T(4,128)S(1)}, f32[4,4,8192]{2,1,0:T(4,128)S(1)}, u32[]{:S(2)}, u32[]{:S(2)}) collective-permute-start(f32[4,4,8192]{2,1,0:T(4,128)S(1)} %get-tuple-element.45), channel_id=1, source_target_pairs={{0,1},{1,2},{2,3},{3,4},{4,5},{5,6},{6,7},{7,8},{8,9},{9,10},{10,1... | collective-permute-start | bytes 1572872 | tf_op jit(solution)/shard_map/ppermute | solution.py:409
  175.5 57.6 %all-to-all-start.2 = ((f32[16,4,16,512]{3,2,1,0:T(8,128)}), f32[16,4,16,512]{3,2,1,0:T(8,128)}, u32[]{:S(2)}, u32[]{:S(2)}) async-start(f32[16,4,16,512]{3,2,1,0:T(8,128)} %ranges.5), calls=%async_computation.2 | async-start | bytes 4194304 | tf_op jit(solution)/shard_map/all_to_all | solution.py:416
  185.8 3.0 %copy-start.3 = (bf16[2304,1536]{1,0:T(8,128)(2,1)S(1)}, bf16[2304,1536]{1,0:T(8,128)(2,1)}, u32[]{:S(2)}) copy-start(bf16[2304,1536]{1,0:T(8,128)(2,1)} %copy-done.2) | copy-start | bytes 21233668
  230.8 2.1 copy-start
  233.1 3.0 %copy-start.4 = (bf16[2304,1536]{1,0:T(8,128)(2,1)S(1)}, bf16[2304,1536]{1,0:T(8,128)(2,1)}, u32[]{:S(2)}) copy-start(bf16[2304,1536]{1,0:T(8,128)(2,1)} %copy-done.2) | copy-start | bytes 21233668
  236.1 19.0 %copy-start.1 = (f32[4,32,8192]{2,1,0:T(8,128)S(1)}, f32[4,32,8192]{2,1,0:T(8,128)}, u32[]{:S(2)}) copy-start(f32[4,32,8192]{2,1,0:T(8,128)} %copy-done) | copy-start | bytes 12582916

commit v3 on v2

--- a/solution.py
+++ b/solution.py
@@ -37,11 +37,14 @@
 
 def table_kernel(plan, offs_ref, lengths_ref, *refs):
     outs, scratch = refs[:-1], refs[-1]
+    deepest = max(item[3] for item in plan)
+    lines = {row: chirp_lines(lengths_ref[row], deepest) for row in {item[0] for item in plan}}
     for (row, shifted, lead, depth, starts), out in zip(plan, outs):
         cols = 8 * len(starts)
         base = lead - offs_ref[1] if shifted else lead
         uniform = len(starts) > 8 and all(start == 8 * k for k, start in enumerate(starts))
-        for part, line in enumerate(chirp_lines(lengths_ref[row], depth)):
+        for part, line in enumerate(lines[row]):
+            line = line[:, 0:depth]
             if uniform:
                 held = line
 
@@ -55,7 +58,7 @@
                     moved = pltpu.roll(line, base + start, 1)
                     scratch[part * cols + 8 * k : part * cols + 8 * k + 8, 0:depth] = moved
 
-        @pl.loop(0, depth // HALF)
+        @pl.loop(0, depth // HALF, unroll=2)
         def _(k):
             at = pl.ds(pl.multiple_of(k * HALF, HALF), HALF)
             turned = scratch[0 : 2 * cols, at].T

time: 262 us -> 260 us (level)
  Pallas kernels: 170 us -> 165 us
  waiting for transfers between devices: 52.7 us -> 55.7 us
    pallas_call x3, Pallas kernels: 25 us -> 19.7 us  [make_tables(): pl.pallas_call(functools.partial(table_kernel, plan), out_shape=[jax.Shap...]
    all_to_all x3, waiting for transfers between devices: 41.7 us -> 44.7 us  [exchange(): return lax.all_to_all(value, 'az', split_axis=0, concat_axis=0, tiled=True)]
  transfers between devices with their start and end apart: 5 -> 5, of which waited for: 4 -> 4; matrix products, arithmetic and copies ran while one was open for 0% -> 0% of each run, Pallas kernels for 47% -> 46%
where the time goes in v3:
time: 260 us; the launch traced here: 258 us
  Pallas kernels  165 us (63%)
  waiting for transfers between devices  55.7 us (21%)
  starting transfers between devices  27.5 us (11%)
  local copies, waits for them, and re-layouts  9.62 us (4%)
    pallas_call x3, Pallas kernels, azimuth_focus(): pl.pallas_call(functools.partial(azimuth_kernel, depth, group), out_shape...  73.6 us
    pallas_call x3, Pallas kernels, range_focus(): pl.pallas_call(functools.partial(range_kernel, plan, windows, share, grou...  60.4 us
    all_to_all x3, waiting for transfers between devices, exchange(): return lax.all_to_all(value, 'az', split_axis=0, concat_axis=0, tiled=True)  44.7 us
    all_to_all x3, starting transfers between devices, exchange(): return lax.all_to_all(value, 'az', split_axis=0, concat_axis=0, tiled=True)  21.9 us
    pallas_call x3, Pallas kernels, make_tables(): pl.pallas_call(functools.partial(table_kernel, plan), out_shape=[jax.Shap...  19.7 us
    pallas_call x2, Pallas kernels, finish(): pl.pallas_call(kernel, grid=(lines_all // block,), out_shape=[jax.ShapeDt...  11.1 us
    ppermute x1, waiting for transfers between devices, bordering(): return (below, lax.ppermute(part[:, 0:4], 'az', down))  11 us
    unnamed x18, local copies, waits for them, and re-layouts  9.44 us
  transfers between devices with their start and end apart: 5, of which 4 were waited for; matrix products, arithmetic and copies ran while one was open for 0% of the time, Pallas kernels for 46%

profile of v3, /device:TPU:17, one launch (start us, length us, event | category | flops | bytes accessed | tf_op | source)
XLA Modules:
  0.0 258.4 jit_solution(11056043446444202092)
XLA Ops:
  0.6 5.3 %tables.3 = (bf16[2304,256]{1,0:T(8,128)(2,1)}, bf16[2560,256]{1,0:T(8,128)(2,1)}) custom-call(s32[2]{0:T(128)} %offs_ref.13, s32[2]{0:T(128)} %lengths_ref.5), custom_call_target="tpu_custom_call" | custom-call | flops 498073600 | bytes 2490368 | tf_op jit(solution)/shard_map/tables/pallas_call | solution.py:81
  5.9 15.4 %ranges.3 = f32[16,4,16,512]{3,2,1,0:T(8,128)} custom-call(s32[2]{0:T(128)} %offs_ref.13, bf16[2,512,8192]{2,1,0:T(8,128)(2,1)} %first_ref.5, bf16[2,512,8192]{2,1,0:T(8,128)(2,1)} %second_ref.5, bf16[2304,256]{1,0:T(8,128)(2,1)} %get-tuple-element.23.refs_0_, bf16[2560,256]{1,0:T(8,128)(2,1)} %get-tuple-element.24.refs_1_), custom_call_target="tpu_custom_call" | custom-call | flops 10200547328 | bytes 16777216 | tf_op jit(solution)/shard_map/ranges/pallas_call | solution.py:151
  21.3 6.5 %all-to-all-start = ((f32[16,4,16,512]{3,2,1,0:T(8,128)}), f32[16,4,16,512]{3,2,1,0:T(8,128)S(1)}, u32[]{:S(2)}, u32[]{:S(2)}) async-start(f32[16,4,16,512]{3,2,1,0:T(8,128)} %ranges.3), calls=%async_computation | async-start | bytes 4194304 | tf_op jit(solution)/shard_map/all_to_all | solution.py:419
  27.8 5.4 %tables.4 = (bf16[2432,256]{1,0:T(8,128)(2,1)}, bf16[2688,256]{1,0:T(8,128)(2,1)}) custom-call(s32[2]{0:T(128)} %offs_ref.13, s32[2]{0:T(128)} %lengths_ref.5), custom_call_target="tpu_custom_call" | custom-call | flops 524288000 | bytes 2621440 | tf_op jit(solution)/shard_map/tables/pallas_call | solution.py:81
  33.2 26.1 %ranges.4 = f32[16,4,32,512]{3,2,1,0:T(8,128)} custom-call(s32[2]{0:T(128)} %offs_ref.13, bf16[2,512,8192]{2,1,0:T(8,128)(2,1)} %first_ref.5, bf16[2,512,8192]{2,1,0:T(8,128)(2,1)} %second_ref.5, bf16[2432,256]{1,0:T(8,128)(2,1)} %get-tuple-element.26.refs_0_, bf16[2688,256]{1,0:T(8,128)(2,1)} %get-tuple-element.27.refs_1_), custom_call_target="tpu_custom_call" | custom-call | flops 20401094656 | bytes 16777216 | tf_op jit(solution)/shard_map/ranges/pallas_call | solution.py:151
  59.2 15.6 %all-to-all-done.got_ref = f32[16,4,16,512]{3,2,1,0:T(8,128)S(1)} async-done(((f32[16,4,16,512]{3,2,1,0:T(8,128)}), f32[16,4,16,512]{3,2,1,0:T(8,128)S(1)}, u32[]{:S(2)}, u32[]{:S(2)}) %all-to-all-start) | async-done | bytes 2097184 | tf_op jit(solution)/shard_map/all_to_all | solution.py:419
  74.8 0.0 copy-start.5
  74.8 1.3 copy-done.5
  76.1 5.2 %all-to-all-start.1 = ((f32[16,4,32,512]{3,2,1,0:T(8,128)}), f32[16,4,32,512]{3,2,1,0:T(8,128)}, u32[]{:S(2)}, u32[]{:S(2)}) async-start(f32[16,4,32,512]{3,2,1,0:T(8,128)} %ranges.4), calls=%async_computation.1 | async-start | bytes 8388608 | tf_op jit(solution)/shard_map/all_to_all | solution.py:419
  81.3 0.0 copy-start.7
  81.3 0.0 copy-start.8
  81.3 18.9 %ranges.5 = f32[16,4,16,512]{3,2,1,0:T(8,128)} custom-call(s32[2]{0:T(128)} %offs_ref.13, bf16[2,512,8192]{2,1,0:T(8,128)(2,1)} %first_ref.5, bf16[2,512,8192]{2,1,0:T(8,128)(2,1)} %second_ref.5, bf16[2432,256]{1,0:T(8,128)(2,1)} %get-tuple-element.26.refs_0_, bf16[2688,256]{1,0:T(8,128)(2,1)} %get-tuple-element.27.refs_1_), custom_call_target="tpu_custom_call" | custom-call | flops 10200547328 | bytes 16777216 | tf_op jit(solution)/shard_map/ranges/pallas_call | solution.py:151
  100.2 0.0 copy-done.7
  100.2 0.0 copy-done.8
  100.2 0.0 copy-start.6
  100.2 9.1 %tables.5.table = bf16[2304,1536]{1,0:T(8,128)(2,1)S(1)} custom-call(s32[2]{0:T(128)S(1)} %copy-done.7, s32[2]{0:T(128)S(1)} %copy-done.8), custom_call_target="tpu_custom_call" | custom-call | flops 1415577600 | bytes 7077888 | tf_op jit(solution)/shard_map/tables/pallas_call | solution.py:81
  109.3 0.0 copy-done.6
  109.3 0.0 copy-start.2
  109.3 18.2 %azimuths.3.refs_2_.refs_6_ = f32[4,16,8192]{2,1,0:T(8,128)S(1)} custom-call(s32[2]{0:T(128)S(1)} %copy-done.7, f32[16,4,16,512]{3,2,1,0:T(8,128)S(1)} %copy-done.6, bf16[2304,1536]{1,0:T(8,128)(2,1)S(1)} %tables.5.table), custom_call_target="tpu_custom_call" | custom-call | flops 10871635968 | bytes 8388608 | tf_op jit(solution)/shard_map/azimuths/pallas_call | solution.py:251
  127.6 0.0 copy-done.2
  127.6 0.2 fusion
  127.8 2.4 collective-permute-start.1
  130.1 3.2 %collective-permute-start = (f32[4,4,8192]{2,1,0:T(4,128)S(1)}, f32[4,4,8192]{2,1,0:T(4,128)S(1)}, u32[]{:S(2)}, u32[]{:S(2)}) collective-permute-start(f32[4,4,8192]{2,1,0:T(4,128)S(1)} %get-tuple-element.45), channel_id=1, source_target_pairs={{0,1},{1,2},{2,3},{3,4},{4,5},{5,6},{6,7},{7,8},{8,9},{9,10},{10,1... | collective-permute-start | bytes 1572872 | tf_op jit(solution)/shard_map/ppermute | solution.py:412
  133.4 11.0 %collective-permute-done.1.refs_1_ = f32[4,4,8192]{2,1,0:T(4,128)S(1)} collective-permute-done((f32[4,4,8192]{2,1,0:T(4,128)S(1)}, f32[4,4,8192]{2,1,0:T(4,128)S(1)}, u32[]{:S(2)}, u32[]{:S(2)}) %collective-permute-start.1) | collective-permute-done | bytes 524320 | tf_op jit(solution)/shard_map/ppermute | solution.py:413
  144.4 0.0 collective-permute-done.refs_0_
  144.4 29.0 %all-to-all-done.1.got_ref = f32[16,4,32,512]{3,2,1,0:T(8,128)} async-done(((f32[16,4,32,512]{3,2,1,0:T(8,128)}), f32[16,4,32,512]{3,2,1,0:T(8,128)}, u32[]{:S(2)}, u32[]{:S(2)}) %all-to-all-start.1) | async-done | bytes 4194336 | tf_op jit(solution)/shard_map/all_to_all | solution.py:419
  173.4 10.3 %all-to-all-start.2 = ((f32[16,4,16,512]{3,2,1,0:T(8,128)}), f32[16,4,16,512]{3,2,1,0:T(8,128)}, u32[]{:S(2)}, u32[]{:S(2)}) async-start(f32[16,4,16,512]{3,2,1,0:T(8,128)} %ranges.5), calls=%async_computation.2 | async-start | bytes 4194304 | tf_op jit(solution)/shard_map/all_to_all | solution.py:419
  183.7 0.0 copy-start.3
  183.7 3.0 %copy-done.3 = bf16[2304,1536]{1,0:T(8,128)(2,1)S(1)} copy-done((bf16[2304,1536]{1,0:T(8,128)(2,1)S(1)}, bf16[2304,1536]{1,0:T(8,128)(2,1)}, u32[]{:S(2)}) %copy-start.3) | copy-done | bytes 7077912
  186.7 36.4 %azimuths.4.refs_3_.refs_4_.refs_5_.refs_6_.refs_2_ = f32[4,32,8192]{2,1,0:T(8,128)S(1)} custom-call(s32[2]{0:T(128)S(1)} %copy-done.7, f32[16,4,32,512]{3,2,1,0:T(8,128)} %all-to-all-done.1.got_ref, bf16[2304,1536]{1,0:T(8,128)(2,1)S(1)} %copy-done.3), custom_call_target="tpu_custom_call" | custom-call | flops 21743271936 | bytes 8388608 | tf_op jit(solution)/shard_map/azimuths/pallas_call | solution.py:251
  223.1 5.5 %finish.2 = (f32[2,64,8192]{2,1,0:T(8,128)}, f32[64,8192]{1,0:T(8,128)}) custom-call(f32[4,4,8192]{2,1,0:T(4,128)S(1)} %collective-permute-done.refs_0_, f32[4,4,8192]{2,1,0:T(4,128)S(1)} %collective-permute-done.1.refs_1_, f32[4,16,8192]{2,1,0:T(8,128)S(1)} %azimuths.3.refs_2_.refs_6_, f32[4,32,8192]{2,1,0:T(8,128)S(1)} %azimuths.4.refs_3_.refs_4_.refs_5_.refs_6_.refs_2_, ...), custom_call_target="tpu_custom_call" | custom-call | flops 786432000 | bytes 16777216 | tf_op jit(solution)/shard_map/finish/pallas_call | solution.py:303
  228.6 0.0 copy-start
  228.6 2.1 copy-done
  230.7 0.1 all-to-all-done.2.got_ref
  230.9 0.0 copy-start.4
  230.9 3.0 %copy-done.4 = bf16[2304,1536]{1,0:T(8,128)(2,1)S(1)} copy-done((bf16[2304,1536]{1,0:T(8,128)(2,1)S(1)}, bf16[2304,1536]{1,0:T(8,128)(2,1)}, u32[]{:S(2)}) %copy-start.4) | copy-done | bytes 7077912
  233.9 0.0 copy-start.1
  233.9 19.0 %azimuths.5.refs_4_.refs_5_ = f32[4,16,8192]{2,1,0:T(8,128)S(1)} custom-call(s32[2]{0:T(128)S(1)} %copy-done.7, f32[16,4,16,512]{3,2,1,0:T(8,128)} %all-to-all-done.2.got_ref, bf16[2304,1536]{1,0:T(8,128)(2,1)S(1)} %copy-done.4), custom_call_target="tpu_custom_call" | custom-call | flops 10871635968 | bytes 8388608 | tf_op jit(solution)/shard_map/azimuths/pallas_call | solution.py:251
  252.9 0.0 copy-done.1
  252.9 5.6 %finish.3 = (f32[2,64,8192]{2,1,0:T(8,128)}, f32[64,8192]{1,0:T(8,128)}) custom-call(f32[4,4,8192]{2,1,0:T(4,128)S(1)} %collective-permute-done.refs_0_, f32[4,4,8192]{2,1,0:T(4,128)S(1)} %collective-permute-done.1.refs_1_, f32[4,32,8192]{2,1,0:T(8,128)S(1)} %copy-done.1, ...), custom_call_target="tpu_custom_call", output_to_operand_aliasing={{0}: (7, {}), {1}: (8, {})} | custom-call | flops 786432000 | bytes 16777216 | tf_op jit(solution)/shard_map/finish/pallas_call | solution.py:303
Async XLA Ops:
  21.3 53.5 %all-to-all-start = ((f32[16,4,16,512]{3,2,1,0:T(8,128)}), f32[16,4,16,512]{3,2,1,0:T(8,128)S(1)}, u32[]{:S(2)}, u32[]{:S(2)}) async-start(f32[16,4,16,512]{3,2,1,0:T(8,128)} %ranges.3), calls=%async_computation | async-start | bytes 4194304 | tf_op jit(solution)/shard_map/all_to_all | solution.py:419
  74.8 1.3 copy-start.5
  76.1 97.2 %all-to-all-start.1 = ((f32[16,4,32,512]{3,2,1,0:T(8,128)}), f32[16,4,32,512]{3,2,1,0:T(8,128)}, u32[]{:S(2)}, u32[]{:S(2)}) async-start(f32[16,4,32,512]{3,2,1,0:T(8,128)} %ranges.4), calls=%async_computation.1 | async-start | bytes 8388608 | tf_op jit(solution)/shard_map/all_to_all | solution.py:419
  81.3 18.9 %copy-start.7 = (s32[2]{0:T(128)S(1)}, s32[2]{0:T(128)}, u32[]{:S(2)}) copy-start(s32[2]{0:T(128)} %offs_ref.13) | copy-start | bytes 28
  81.3 18.9 %copy-start.8 = (s32[2]{0:T(128)S(1)}, s32[2]{0:T(128)}, u32[]{:S(2)}) copy-start(s32[2]{0:T(128)} %lengths_ref.5) | copy-start | bytes 28
  100.2 9.1 %copy-start.6 = (f32[16,4,16,512]{3,2,1,0:T(8,128)S(1)}, f32[16,4,16,512]{3,2,1,0:T(8,128)}, u32[]{:S(2)}) copy-start(f32[16,4,16,512]{3,2,1,0:T(8,128)} %copy-done.5) | copy-start | bytes 6291460
  109.3 18.3 %copy-start.2 = (bf16[2304,1536]{1,0:T(8,128)(2,1)}, bf16[2304,1536]{1,0:T(8,128)(2,1)S(1)}, u32[]{:S(2)}) copy-start(bf16[2304,1536]{1,0:T(8,128)(2,1)S(1)} %tables.5.table) | copy-start | bytes 21233668
  127.8 16.6 %collective-permute-start.1 = (f32[4,4,8192]{2,1,0:T(4,128)S(1)}, f32[4,4,8192]{2,1,0:T(4,128)S(1)}, u32[]{:S(2)}, u32[]{:S(2)}) collective-permute-start(f32[4,4,8192]{2,1,0:T(4,128)S(1)} %get-tuple-element.44), channel_id=1, source_target_pairs={{1,0},{2,1},{3,2},{4,3},{5,4},{6,5},{7,6},{8,7},{9,8},{10,9},{11,1... | collective-permute-start | bytes 1572872 | tf_op jit(solution)/shard_map/ppermute | solution.py:413
  130.1 14.2 %collective-permute-start = (f32[4,4,8192]{2,1,0:T(4,128)S(1)}, f32[4,4,8192]{2,1,0:T(4,128)S(1)}, u32[]{:S(2)}, u32[]{:S(2)}) collective-permute-start(f32[4,4,8192]{2,1,0:T(4,128)S(1)} %get-tuple-element.45), channel_id=1, source_target_pairs={{0,1},{1,2},{2,3},{3,4},{4,5},{5,6},{6,7},{7,8},{8,9},{9,10},{10,1... | collective-permute-start | bytes 1572872 | tf_op jit(solution)/shard_map/ppermute | solution.py:412
  173.4 57.5 %all-to-all-start.2 = ((f32[16,4,16,512]{3,2,1,0:T(8,128)}), f32[16,4,16,512]{3,2,1,0:T(8,128)}, u32[]{:S(2)}, u32[]{:S(2)}) async-start(f32[16,4,16,512]{3,2,1,0:T(8,128)} %ranges.5), calls=%async_computation.2 | async-start | bytes 4194304 | tf_op jit(solution)/shard_map/all_to_all | solution.py:419
  183.7 3.0 %copy-start.3 = (bf16[2304,1536]{1,0:T(8,128)(2,1)S(1)}, bf16[2304,1536]{1,0:T(8,128)(2,1)}, u32[]{:S(2)}) copy-start(bf16[2304,1536]{1,0:T(8,128)(2,1)} %copy-done.2) | copy-start | bytes 21233668
  228.6 2.1 copy-start
  230.9 3.0 %copy-start.4 = (bf16[2304,1536]{1,0:T(8,128)(2,1)S(1)}, bf16[2304,1536]{1,0:T(8,128)(2,1)}, u32[]{:S(2)}) copy-start(bf16[2304,1536]{1,0:T(8,128)(2,1)} %copy-done.2) | copy-start | bytes 21233668
  233.9 19.0 %copy-start.1 = (f32[4,32,8192]{2,1,0:T(8,128)S(1)}, f32[4,32,8192]{2,1,0:T(8,128)}, u32[]{:S(2)}) copy-start(f32[4,32,8192]{2,1,0:T(8,128)} %copy-done) | copy-start | bytes 12582916
